TPU v7x, 32 devices: a whole 2x2x4 slice. The times are simulated.
32 devices in a mesh: rep: 2 (over y), dp: 16 (over z, x, core).
Axes of the slice: x: 2, y: 2, z: 4, core: 2. Of those that a mesh axis runs over, the one named last changes fastest.
Arguments:
- hidden: bfloat16 [256, 2, 3584], P(('rep', 'dp')), may hold values from -96 to 96
- lm_head: bfloat16 [3584, 12288], P(None, ('rep', 'dp')), may hold values from -0.3125 to 0.3125
- reward_head: bfloat16 [3584], replicated, may hold values from -0.09375 to 0.09375
- target_ids: int32 [256, 2], P(('rep', 'dp')), may hold values from 0 to 12287
- lengths: int32 [256], P(('rep', 'dp')), may hold values from 1 to 2
- prompt_ids: int32 [256], P(('rep', 'dp')), may hold values from 0 to 15, as said below
Outputs:
- token_logprobs: float32 [256, 2], P(('rep', 'dp'))
- advantages: float32 [256], P(('rep', 'dp'))
Inputs may be any that keep to these rules, and one draw needn't show every extreme that they name: `prompt_ids`: each prompt id names exactly 16 responses.
All inputs are finite; a program needn't handle non-finite values.
Results may differ from a plain program's by a relative error of at most 0.0003.
Values may be sent and summed in bfloat16 or wider, within the bound.
No kernel may reach another device: no remote copies, remote signals or barrier semaphores. Data moves between devices by JAX's collectives and lax.ppermute only.
A program may use at most 128 MiB of HBM per device.

v0:
```python
import functools

import jax
import jax.numpy as jnp
from jax import lax
from jax.experimental import pallas as pl
from jax.experimental.pallas import tpu as pltpu
from jax.sharding import PartitionSpec as P


GROUP = 16
LANES = 128
ROWS = 256
SMALL = 4 << 20
MARGIN = 3 << 20
AXES = ("rep", "dp")
VMEM = pltpu.VMEM


def bits_of(count):
    return [1 << k for k in range(count.bit_length() - 1)]


class Piece:
    def __init__(self, rows, tiles):
        self.rows = rows
        self.tiles = tiles


def swap(piece, masks, devices):
    pairs = [(i, i ^ masks[i & 1]) for i in range(devices)]
    rows = lax.ppermute(piece.rows, AXES, pairs)
    if masks == (1, 1):
        tiles = [(1 ^ b, 1 ^ a) for a, b in piece.tiles]
    else:
        tiles = [(a ^ masks[0], b ^ masks[1]) for a, b in piece.tiles]
    return Piece(rows, tiles)


def join_kernel(*refs):
    *parts, out_ref = refs
    first = 0
    for part in parts:
        count = part.shape[0]
        out_ref[first : first + count, :] = part[...]
        first += count


def join(*pieces):
    count, width = sum(p.rows.shape[0] for p in pieces), pieces[0].rows.shape[1]
    vmem = pl.BlockSpec(memory_space=VMEM)
    rows = pl.pallas_call(
        join_kernel,
        out_shape=jax.ShapeDtypeStruct((count, width), pieces[0].rows.dtype),
        in_specs=[vmem] * len(pieces),
        out_specs=vmem,
        compiler_params=pltpu.CompilerParams(vmem_limit_bytes=SMALL + 4 * count * width),
        cost_estimate=pl.CostEstimate(flops=count * width, bytes_accessed=4 * count * width, transcendentals=0),
        name="join",
    )(*[p.rows for p in pieces])
    return Piece(rows, sum((p.tiles for p in pieces), []))


def gather(own, rep, dp):
    devices = rep * dp
    inner = bits_of(dp)[1:]
    far, near = inner[-2:], inner[:-2]
    outer = [b * dp for b in bits_of(rep)]
    stages = []
    for k in range(max(len(near), len(outer))):
        pair = near[k : k + 1] + outer[k : k + 1]
        stages += [(pair[0], pair[-1]), (pair[-1], pair[0])][: len(pair)]
    *before, one, two = stages
    for masks in before:
        own = join(own, swap(own, masks, devices))
    z1, z2 = [swap(own, (m, m), devices) for m in far]
    z3 = swap(z2, (far[0], far[0]), devices)
    own_1 = swap(own, one, devices)
    own_3 = swap(own, two, devices)
    own_2 = swap(join(z1, own_1), two, devices)
    near = join(own, z1, own_1, own_3)
    near_1 = swap(z1, one, devices)
    far_1 = swap(z2, one, devices)
    last_1 = swap(z3, one, devices)
    second = join(z2, near_1)
    second_2 = swap(second, two, devices)
    third = join(far_1, z3)
    third_2 = swap(third, two, devices)
    last_2 = swap(last_1, two, devices)
    buckets = [[near, own_2, second], [third, second_2], [last_1, third_2, last_2]]
    return [b + [swap(p, (1, 1), devices) for p in b] for b in buckets]


def iota(shape, axis):
    return lax.broadcasted_iota(jnp.int32, shape, axis)


def prepare_kernel(hidden_ref, names_ref, own_ref):
    resp, window, width = hidden_ref.shape
    tokens = resp * window
    own_ref[:, :width] = hidden_ref[...].reshape(tokens, width)
    lane, row = iota((tokens, resp), 1), iota((tokens, resp), 0)
    ids = names_ref[...]
    mine = jnp.zeros((tokens, resp), jnp.int32)
    for w in range(window):
        mine = jnp.where((row % window == w) & (row // window == lane), ids[w : w + 1, :], mine)
    mine = jnp.sum(mine, axis=1, keepdims=True)
    place = iota((tokens, LANES), 1)
    digits = jnp.where(place == 0, mine & 255, jnp.where(place == 1, (mine >> 8) & 255, mine >> 16))
    digits = jnp.where(place < 3, digits.astype(jnp.float32), 0.0)
    own_ref[:, width:] = digits.astype(jnp.bfloat16)


def moments_kernel(me_ref, own_ref, head_ref, names_ref, weights_ref, sums_ref, member_ref, rewards_ref, *, start, prompts):
    tokens = own_ref.shape[0]
    resp = member_ref.shape[0]
    window = tokens // resp
    wide = sums_ref.shape[1]
    lengths, prompt = names_ref[window : window + 1, :], names_ref[window + 1 : window + 2, :]
    parts = head_ref.shape[0]
    each = jnp.zeros((tokens, LANES), jnp.float32)
    for k in range(parts):
        rows = own_ref[:, k * LANES : (k + 1) * LANES].astype(jnp.float32)
        each += rows * head_ref[k : k + 1, :].astype(jnp.float32)
    each = jnp.sum(each, axis=1, keepdims=True)
    last = iota((tokens, resp), 0) == iota((tokens, resp), 1) * window + lengths - 1
    across = jnp.sum(jnp.where(last, each, 0.0), axis=0, keepdims=True)
    diag = iota((resp, resp), 0) == iota((resp, resp), 1)
    rewards = jnp.sum(jnp.where(diag, across, 0.0), axis=1, keepdims=True)
    named = jnp.sum(jnp.where(diag, prompt, 0), axis=1, keepdims=True)
    lane = iota((resp, wide), 1)
    member_ref[...] = jnp.where(lane == named, 1.0, 0.0)
    first = jnp.where(lane == named + start, rewards, 0.0)
    second = jnp.where(lane == named + (start + prompts), rewards * rewards, 0.0)
    sums_ref[...] = jnp.sum(first + second, axis=0, keepdims=True)
    rewards_ref[...] = jnp.broadcast_to(rewards, rewards_ref.shape)


def stats_block(part, head, base, window, tokens, wide):
    width, vocab = head.shape
    rows = part.shape[0]
    resp = tokens // window
    logits = jnp.dot(part[:, :width], head, preferred_element_type=jnp.float32)
    digits = part[:, width : width + LANES].astype(jnp.float32)
    wanted = digits[:, 0:1] + 256.0 * digits[:, 1:2] + 65536.0 * digits[:, 2:3] - base
    columns = iota((rows, vocab), 1).astype(jnp.float32)
    peak = jnp.max(logits, axis=1, keepdims=True)
    total = jnp.sum(jnp.exp(logits - peak), axis=1, keepdims=True)
    picked = jnp.sum(jnp.where(columns == wanted, logits, 0.0), axis=1, keepdims=True)
    lane, token = iota((rows, wide), 1), iota((rows, wide), 0) % tokens
    slot = (token % window) * resp + token // window
    values = jnp.where(lane == slot, peak, 0.0)
    values = jnp.where(lane == slot + tokens, total, values)
    values = jnp.where(lane == slot + 2 * tokens, picked, values)
    share = max(1, 8 // tokens)
    tile = tokens * share
    values = values.reshape(rows // tile, tile, wide)
    tiles = []
    for k in range(share):
        mine = values
        if share > 1:
            mine = jnp.where(iota(values.shape, 1) // tokens == k, values, 0.0)
        tiles.append(jnp.sum(mine, axis=1))
    return tiles


def stats_kernel(me_ref, head_ref, *refs, window, tokens, marks, early):
    if marks is None:
        pieces, tiles_ref = refs[:-1], refs[-1]
        wide = tiles_ref.shape[2]
    else:
        sums_ref, others, pieces, message_ref, tiles_ref = refs[0], refs[1 : 1 + early], refs[1 + early : -2], refs[-2], refs[-1]
        wide = message_ref.shape[1]
    share = max(1, 8 // tokens)
    tile = tokens * share
    vocab = head_ref.shape[1]
    me = me_ref[0]
    base = (me * vocab).astype(jnp.float32)
    limit = max(8 * tile, ROWS)

    def work(parts, first):
        part = parts[0] if len(parts) == 1 else jnp.concatenate(parts, 0)
        for k, rows in enumerate(stats_block(part, head_ref[...], base, window, tokens, wide)):
            tiles_ref[k, pl.ds(first, rows.shape[0]), :] = rows

    first, small = 0, []
    for piece in pieces:
        count = piece.shape[0]
        if sum(p.shape[0] for p in small) + count > limit and small:
            work([p[...] for p in small], first)
            first += sum(p.shape[0] for p in small) // tile
            small = []
        if count <= limit:
            small.append(piece)
            continue
        for i in range(count // limit):
            work([piece[i * limit : (i + 1) * limit, :]], first)
            first += limit // tile
    if small:
        work([p[...] for p in small], first)
    if marks is None:
        return

    sums = sums_ref[...]
    even = me % 2 == 0
    index = 0
    for ref in (*others, tiles_ref):
        for i in range(ref.shape[1]):
            for k in range(share):
                low, high = marks[index]
                row = me ^ (jnp.where(even, low, high) if low != high else low)
                message_ref[pl.ds(row, 1), :] = ref[k, i : i + 1, :] + sums
                index += 1


def finish_kernel(message_ref, member_ref, rewards_ref, names_ref, logprobs_ref, advantages_ref, *, tokens, prompts):
    window, resp = logprobs_ref.shape
    message = message_ref[...]
    wide = message.shape[1]
    back = lambda x, by: pltpu.roll(x, (wide - by) % wide, 1)
    top = jnp.max(message, axis=0, keepdims=True)
    scaled = back(message, tokens) * jnp.exp(jnp.minimum(message - top, 0.0))
    total = jnp.sum(scaled, axis=0, keepdims=True)
    whole = jnp.sum(message, axis=0, keepdims=True)
    lane = iota((1, wide), 1)
    total = jnp.where(lane < tokens, total, 1.0)
    logprob = back(whole, 2 * tokens) - (top + jnp.log(total))
    for w in range(window):
        row = back(logprob, w * resp)[:, :resp] if w else logprob[:, :resp]
        logprobs_ref[w : w + 1, :] = jnp.where(w < names_ref[window : window + 1, :], row, 0.0)
    means = back(whole, 3 * tokens) * (1.0 / GROUP)
    squares = back(whole, 3 * tokens + prompts) * (1.0 / GROUP)
    scales = jnp.sqrt(jnp.maximum(squares - means * means, 1.0))
    member = member_ref[...] > 0.5
    centre = jnp.sum(jnp.where(member, means, 0.0), axis=1, keepdims=True)
    spread = jnp.sum(jnp.where(member, scales, 0.0), axis=1, keepdims=True)
    advantages = (rewards_ref[:, 0:1] - centre) / spread
    diag = iota((resp, resp), 0) == iota((resp, resp), 1)
    advantages_ref[...] = jnp.sum(jnp.where(diag, advantages, 0.0), axis=0, keepdims=True)


def body(hidden, lm_head, reward_head, target_ids, lengths, prompt_ids):
    resp, window, width = hidden.shape
    vocab = lm_head.shape[1]
    rep, dp = lax.axis_size("rep"), lax.axis_size("dp")
    devices = rep * dp
    me = lax.axis_index("rep") * dp + lax.axis_index("dp")
    me = me.astype(jnp.int32).reshape(1)
    tokens = resp * window
    prompts = resp * devices // GROUP
    wide = -(-(3 * tokens + 2 * prompts) // LANES) * LANES
    share = max(1, 8 // tokens)
    f32 = jnp.float32
    smem = pl.BlockSpec(memory_space=pltpu.SMEM)
    vmem = pl.BlockSpec(memory_space=VMEM)

    names = jnp.concatenate([target_ids.T, lengths.reshape(1, resp), prompt_ids.reshape(1, resp)], 0)
    own = pl.pallas_call(
        prepare_kernel,
        out_shape=jax.ShapeDtypeStruct((tokens, width + LANES), jnp.bfloat16),
        compiler_params=pltpu.CompilerParams(vmem_limit_bytes=SMALL),
        name="prepare",
    )(hidden, names)
    buckets = gather(Piece(own, [(0, 0)]), rep, dp)

    sums, member, rewards = pl.pallas_call(
        functools.partial(moments_kernel, start=3 * tokens, prompts=prompts),
        out_shape=(
            jax.ShapeDtypeStruct((1, wide), f32),
            jax.ShapeDtypeStruct((resp, wide), f32),
            jax.ShapeDtypeStruct((resp, LANES), f32),
        ),
        in_specs=[smem] + [vmem] * 4,
        out_specs=[vmem] * 3,
        compiler_params=pltpu.CompilerParams(vmem_limit_bytes=SMALL),
        cost_estimate=pl.CostEstimate(flops=10**7, bytes_accessed=2 * hidden.size, transcendentals=0),
        name="moments",
    )(me, own, reward_head.reshape(width // LANES, LANES), names, lm_head)

    marks = [m for b in buckets for p in b for m in p.tiles]

    def stats(bucket, early):
        count = sum(p.rows.shape[0] for p in bucket)
        tiles = (share, count // tokens // share, wide)
        last = early is not None
        given = [sums, *early] if last else []
        cost = pl.CostEstimate(flops=2 * count * lm_head.size, bytes_accessed=2 * lm_head.size, transcendentals=count * vocab)
        return pl.pallas_call(
            functools.partial(stats_kernel, window=window, tokens=tokens, marks=marks if last else None, early=len(given) - 1),
            out_shape=jax.ShapeDtypeStruct((devices, wide) if last else tiles, f32),
            in_specs=[smem] + [vmem] * (1 + len(given) + len(bucket)),
            out_specs=vmem,
            scratch_shapes=[VMEM(tiles, f32)] if last else [],
            compiler_params=pltpu.CompilerParams(vmem_limit_bytes=MARGIN + 2 * lm_head.size + 2 * count * (width + LANES)),
            cost_estimate=cost,
            name="stats",
        )(me, lm_head, *given, *[p.rows for p in bucket])

    early = [stats(b, None) for b in buckets[:-1]]
    message = stats(buckets[-1], early)
    answer = lax.all_to_all(message, AXES, 0, 0, tiled=True)
    logprobs, advantages = pl.pallas_call(
        functools.partial(finish_kernel, tokens=tokens, prompts=prompts),
        out_shape=(
            jax.ShapeDtypeStruct((window, resp), f32),
            jax.ShapeDtypeStruct((1, resp), f32),
        ),
        compiler_params=pltpu.CompilerParams(vmem_limit_bytes=SMALL),
        name="finish",
    )(answer, member, rewards, names)
    return (logprobs.T, advantages.reshape(resp))


def solution(mesh):
    in_specs = (
        P(("rep", "dp"), None, None),
        P(None, ("rep", "dp")),
        P(),
        P(("rep", "dp"), None),
        P(("rep", "dp")),
        P(("rep", "dp")),
    )
    out_specs = (P(("rep", "dp"), None), P(("rep", "dp")))
    return jax.shard_map(body, mesh=mesh, in_specs=in_specs, out_specs=out_specs, check_vma=False)
```

profile of v0, /device:TPU:0, one launch (start us, length us, event | category | flops | bytes accessed | tf_op | source)
XLA Modules:
  0.0 53.8 jit_solution(5303890998037892019)
XLA Ops:
  0.6 0.7 %pad_add_fusion.names_ref = s32[4,8]{1,0:T(4,128)S(1)} fusion(s32[1,8]{1,0:T(1,128)} %bitcast.15, s32[1,8]{1,0:T(1,128)} %bitcast.16, s32[2,8]{1,0:T(2,128)} %bitcast.14), kind=kLoop, calls=%fused_computation | loop fusion | flops 64 | bytes 256 | tf_op jit(solution)/shard_map/concatenate | solution.py:257
  1.4 0.9 %copy-done.2 = bf16[8,2,3584]{2,1,0:T(2,128)(2,1)S(1)} copy-done((bf16[8,2,3584]{2,1,0:T(2,128)(2,1)S(1)}, bf16[8,2,3584]{2,1,0:T(2,128)(2,1)}, u32[]{:S(2)}) %copy-start.2) | copy-done | bytes 114712
  2.3 0.1 prepare.1.own_ref.refs_0_
  2.4 3.1 %collective-permute-start = (bf16[16,3712]{1,0:T(8,128)(2,1)S(1)}, bf16[16,3712]{1,0:T(8,128)(2,1)S(1)}, u32[]{:S(2)}, u32[]{:S(2)}) collective-permute-start(bf16[16,3712]{1,0:T(8,128)(2,1)S(1)} %prepare.1.own_ref.refs_0_), channel_id=1, source_target_pairs={{0,4},{1,5},{2,6},{3,7},{4,0},{5,1},{6,2},{7,3},{8,12},{9,13},{10,... | collective-permute-start | bytes 356360 | tf_op jit(solution)/shard_map/ppermute | solution.py:32
  5.5 1.5 %collective-permute-start.1 = (bf16[16,3712]{1,0:T(8,128)(2,1)S(1)}, bf16[16,3712]{1,0:T(8,128)(2,1)S(1)}, u32[]{:S(2)}, u32[]{:S(2)}) collective-permute-start(bf16[16,3712]{1,0:T(8,128)(2,1)S(1)} %prepare.1.own_ref.refs_0_), channel_id=1, source_target_pairs={{0,2},{1,17},{2,0},{3,19},{4,6},{5,21},{6,4},{7,23},{8,10},{9,25},... | collective-permute-start | bytes 356360 | tf_op jit(solution)/shard_map/ppermute | solution.py:32
  7.0 2.6 %collective-permute-start.4 = (bf16[16,3712]{1,0:T(8,128)(2,1)S(1)}, bf16[16,3712]{1,0:T(8,128)(2,1)S(1)}, u32[]{:S(2)}, u32[]{:S(2)}) collective-permute-start(bf16[16,3712]{1,0:T(8,128)(2,1)S(1)} %prepare.1.own_ref.refs_0_), channel_id=1, source_target_pairs={{0,8},{1,9},{2,10},{3,11},{4,12},{5,13},{6,14},{7,15},{8,0},{9,1},... | collective-permute-start | bytes 356360 | tf_op jit(solution)/shard_map/ppermute | solution.py:32
  9.6 1.5 %collective-permute-start.2 = (bf16[16,3712]{1,0:T(8,128)(2,1)S(1)}, bf16[16,3712]{1,0:T(8,128)(2,1)S(1)}, u32[]{:S(2)}, u32[]{:S(2)}) collective-permute-start(bf16[16,3712]{1,0:T(8,128)(2,1)S(1)} %prepare.1.own_ref.refs_0_), channel_id=1, source_target_pairs={{0,16},{1,3},{2,18},{3,1},{4,20},{5,7},{6,22},{7,5},{8,24},{9,11},... | collective-permute-start | bytes 356360 | tf_op jit(solution)/shard_map/ppermute | solution.py:32
  11.1 0.0 collective-permute-done.refs_1_.refs_0_
  11.1 0.0 collective-permute-done.1.refs_2_.refs_1_
  11.1 1.0 %collective-permute-start.3 = (bf16[32,3712]{1,0:T(8,128)(2,1)S(1)}, bf16[32,3712]{1,0:T(8,128)(2,1)S(1)}, u32[]{:S(2)}, u32[]{:S(2)}) collective-permute-start(bf16[32,3712]{1,0:T(8,128)(2,1)S(1)} %join.5), channel_id=1, source_target_pairs={{0,16},{1,3},{2,18},{3,1},{4,20},{5,7},{6,22},{7,5},{8,24},{9,11},... | collective-permute-start | bytes 712712 | tf_op jit(solution)/shard_map/ppermute | solution.py:32
  12.1 1.5 %collective-permute-start.5 = (bf16[16,3712]{1,0:T(8,128)(2,1)S(1)}, bf16[16,3712]{1,0:T(8,128)(2,1)S(1)}, u32[]{:S(2)}, u32[]{:S(2)}) collective-permute-start(bf16[16,3712]{1,0:T(8,128)(2,1)S(1)} %collective-permute-done.refs_1_.refs_0_), channel_id=1, source_target_pairs={{0,2},{1,17},{2,0},{3,19},{4,6},{5,21},{6,4},{7,23},{8,10},{9,25},... | collective-permute-start | bytes 356360 | tf_op jit(solution)/shard_map/ppermute | solution.py:32
  13.6 1.3 %collective-permute-done.4.refs_0_ = bf16[16,3712]{1,0:T(8,128)(2,1)S(1)} collective-permute-done((bf16[16,3712]{1,0:T(8,128)(2,1)S(1)}, bf16[16,3712]{1,0:T(8,128)(2,1)S(1)}, u32[]{:S(2)}, u32[]{:S(2)}) %collective-permute-start.4) | collective-permute-done | bytes 118816 | tf_op jit(solution)/shard_map/ppermute | solution.py:32
  14.8 1.5 %collective-permute-start.9 = (bf16[16,3712]{1,0:T(8,128)(2,1)S(1)}, bf16[16,3712]{1,0:T(8,128)(2,1)S(1)}, u32[]{:S(2)}, u32[]{:S(2)}) collective-permute-start(bf16[16,3712]{1,0:T(8,128)(2,1)S(1)} %collective-permute-done.4.refs_0_), channel_id=1, source_target_pairs={{0,2},{1,17},{2,0},{3,19},{4,6},{5,21},{6,4},{7,23},{8,10},{9,25},... | collective-permute-start | bytes 356360 | tf_op jit(solution)/shard_map/ppermute | solution.py:32
  16.3 0.0 collective-permute-start.10
  16.3 0.0 collective-permute-done.2.refs_3_
  16.4 0.1 collective-permute-start.6
  16.5 0.4 collective-permute-done.5.refs_1_
  16.9 0.1 collective-permute-start.8
  17.0 2.6 %collective-permute-done.9.refs_0_ = bf16[16,3712]{1,0:T(8,128)(2,1)S(1)} collective-permute-done((bf16[16,3712]{1,0:T(8,128)(2,1)S(1)}, bf16[16,3712]{1,0:T(8,128)(2,1)S(1)}, u32[]{:S(2)}, u32[]{:S(2)}) %collective-permute-start.9) | collective-permute-done | bytes 118816 | tf_op jit(solution)/shard_map/ppermute | solution.py:32
  19.7 1.1 %collective-permute-start.11 = (bf16[32,3712]{1,0:T(8,128)(2,1)S(1)}, bf16[32,3712]{1,0:T(8,128)(2,1)S(1)}, u32[]{:S(2)}, u32[]{:S(2)}) collective-permute-start(bf16[32,3712]{1,0:T(8,128)(2,1)S(1)} %join.6.refs_2_), channel_id=1, source_target_pairs={{0,16},{1,3},{2,18},{3,1},{4,20},{5,7},{6,22},{7,5},{8,24},{9,11},... | collective-permute-start | bytes 712712 | tf_op jit(solution)/shard_map/ppermute | solution.py:32
  20.8 0.4 collective-permute-done.10.refs_1_
  21.2 0.7 %collective-permute-start.15 = (bf16[32,3712]{1,0:T(8,128)(2,1)S(1)}, bf16[32,3712]{1,0:T(8,128)(2,1)S(1)}, u32[]{:S(2)}, u32[]{:S(2)}) collective-permute-start(bf16[32,3712]{1,0:T(8,128)(2,1)S(1)} %join.7.refs_0_), channel_id=1, source_target_pairs={{0,16},{1,3},{2,18},{3,1},{4,20},{5,7},{6,22},{7,5},{8,24},{9,11},... | collective-permute-start | bytes 712712 | tf_op jit(solution)/shard_map/ppermute | solution.py:32
  21.9 0.0 collective-permute-done.3.refs_1_
  21.9 1.4 %collective-permute-start.14 = (bf16[16,3712]{1,0:T(8,128)(2,1)S(1)}, bf16[16,3712]{1,0:T(8,128)(2,1)}, u32[]{:S(2)}, u32[]{:S(2)}) collective-permute-start(bf16[16,3712]{1,0:T(8,128)(2,1)S(1)} %collective-permute-done.10.refs_1_), channel_id=1, source_target_pairs={{0,2},{1,17},{2,0},{3,19},{4,6},{5,21},{6,4},{7,23},{8,10},{9,25},... | collective-permute-start | bytes 356360 | tf_op jit(solution)/shard_map/ppermute | solution.py:32
  23.3 4.8 %collective-permute-done.14.refs_3_ = bf16[16,3712]{1,0:T(8,128)(2,1)} collective-permute-done((bf16[16,3712]{1,0:T(8,128)(2,1)S(1)}, bf16[16,3712]{1,0:T(8,128)(2,1)}, u32[]{:S(2)}, u32[]{:S(2)}) %collective-permute-start.14) | collective-permute-done | bytes 118816 | tf_op jit(solution)/shard_map/ppermute | solution.py:32
  28.1 0.0 collective-permute-start.7
  28.1 0.0 collective-permute-done.8.refs_5_
  28.1 0.7 %collective-permute-start.16 = (bf16[16,3712]{1,0:T(8,128)(2,1)}, bf16[16,3712]{1,0:T(8,128)(2,1)}, u32[]{:S(2)}, u32[]{:S(2)}) collective-permute-start(bf16[16,3712]{1,0:T(8,128)(2,1)} %collective-permute-done.14.refs_3_), channel_id=1, source_target_pairs={{0,16},{1,3},{2,18},{3,1},{4,20},{5,7},{6,22},{7,5},{8,24},{9,11},... | collective-permute-start | bytes 356360 | tf_op jit(solution)/shard_map/ppermute | solution.py:32
  28.8 0.0 collective-permute-done.11.refs_1_
  28.8 0.7 %collective-permute-start.12 = (bf16[32,3712]{1,0:T(8,128)(2,1)S(1)}, bf16[32,3712]{1,0:T(8,128)(2,1)S(1)}, u32[]{:S(2)}, u32[]{:S(2)}) collective-permute-start(bf16[32,3712]{1,0:T(8,128)(2,1)S(1)} %join.7.refs_0_), channel_id=1, source_target_pairs={{0,1},{1,0},{2,3},{3,2},{4,5},{5,4},{6,7},{7,6},{8,9},{9,8},{10,11... | collective-permute-start | bytes 712712 | tf_op jit(solution)/shard_map/ppermute | solution.py:32
  29.4 0.2 collective-permute-done.15.refs_4_
  29.6 0.0 collective-permute-start.13
  29.6 3.6 %collective-permute-done.16.refs_5_ = bf16[16,3712]{1,0:T(8,128)(2,1)} collective-permute-done((bf16[16,3712]{1,0:T(8,128)(2,1)}, bf16[16,3712]{1,0:T(8,128)(2,1)}, u32[]{:S(2)}, u32[]{:S(2)}) %collective-permute-start.16) | collective-permute-done | bytes 118816 | tf_op jit(solution)/shard_map/ppermute | solution.py:32
  33.2 0.0 collective-permute-start.18
  33.2 0.0 collective-permute-done.6.refs_3_
  33.2 0.5 collective-permute-start.17
  33.8 0.1 collective-permute-start.19
  33.8 1.8 %copy-done = bf16[3584,384]{1,0:T(8,128)(2,1)S(1)} copy-done((bf16[3584,384]{1,0:T(8,128)(2,1)S(1)}, bf16[3584,384]{1,0:T(8,128)(2,1)}, u32[]{:S(2)}) %copy-start) | copy-done | bytes 2752536
  35.6 0.7 %copy-done.3 = bf16[3584]{0:T(1024)(128)(2,1)S(1)} copy-done((bf16[3584]{0:T(1024)(128)(2,1)S(1)}, bf16[3584]{0:T(1024)(128)(2,1)}, u32[]{:S(2)}) %copy-start.3) | copy-done | bytes 7192
  36.3 0.2 moments.1
  36.5 1.6 %copy-done.1 = bf16[3584,384]{1,0:T(8,128)(2,1)S(1)} copy-done((bf16[3584,384]{1,0:T(8,128)(2,1)S(1)}, bf16[3584,384]{1,0:T(8,128)(2,1)}, u32[]{:S(2)}) %copy-start.1) | copy-done | bytes 2752536
  38.1 1.3 %stats.3.refs_1_ = f32[1,16,128]{2,1,0:T(8,128)S(1)} custom-call(s32[1]{0:T(128)} %bitcast.me_ref, bf16[3584,384]{1,0:T(8,128)(2,1)S(1)} %copy-done.1, bf16[64,3712]{1,0:T(8,128)(2,1)S(1)} %join.4.refs_0_, bf16[32,3712]{1,0:T(8,128)(2,1)S(1)} %collective-permute-done.3.refs_1_, bf16[32,3712]{1,0:T(8,128)(2,1)S(1)} %join.6.refs_2_, ...), custom_call_target="tpu_custom_call" | custom-call | flops 704643072 | bytes 2752512 | tf_op jit(solution)/shard_map/stats/pallas_call | solution.py:288
  39.4 0.8 %stats.4.refs_2_ = f32[1,8,128]{2,1,0:T(8,128)S(1)} custom-call(s32[1]{0:T(128)} %bitcast.me_ref, bf16[3584,384]{1,0:T(8,128)(2,1)S(1)} %copy-done.1, bf16[32,3712]{1,0:T(8,128)(2,1)S(1)} %join.7.refs_0_, bf16[32,3712]{1,0:T(8,128)(2,1)S(1)} %collective-permute-done.11.refs_1_, bf16[32,3712]{1,0:T(8,128)(2,1)S(1)} %collective-permute-done.12.refs_2_, ...), custom_call_target="tpu_custom_call" | custom-call | flops 352321536 | bytes 2752512 | tf_op jit(solution)/shard_map/stats/pallas_call | solution.py:288
  40.3 0.0 collective-permute-done.19.refs_8_
  40.3 0.0 collective-permute-done.18.refs_7_
  40.3 1.9 %stats.5 = f32[32,128]{1,0:T(8,128)S(1)} custom-call(s32[1]{0:T(128)} %bitcast.me_ref, bf16[3584,384]{1,0:T(8,128)(2,1)S(1)} %copy-done.1, f32[1,128]{1,0:T(1,128)S(1)} %get-tuple-element.7.refs_0_, f32[1,16,128]{2,1,0:T(8,128)S(1)} %stats.3.refs_1_, f32[1,8,128]{2,1,0:T(8,128)S(1)} %stats.4.refs_2_, bf16[16,3712]{1,0:T(8,128)(2,1)} %collective-permute-done.14.refs_3_, ...), custom_call_target="tpu_custom_call" | custom-call | flops 352321536 | bytes 2752512 | tf_op jit(solution)/shard_map/stats/pallas_call | solution.py:288
  42.2 10.8 %all_to_all.11 = f32[32,1,128]{2,1,0:T(1,128)S(1)} all-to-all(f32[32,1,128]{2,1,0:T(1,128)S(1)} %bitcast.11), channel_id=1, replica_groups=mesh['rep'=2,'dp'=16] {'rep','dp'}, dimensions={0} | all-to-all | bytes 32768 | tf_op jit(solution)/shard_map/all_to_all | solution.py:301
  53.0 0.8 %finish.1 = (f32[2,8]{1,0:T(2,128)}, f32[1,8]{1,0:T(1,128)}) custom-call(f32[32,128]{1,0:T(8,128)S(1)} %bitcast.12, f32[8,128]{1,0:T(8,128)S(1)} %get-tuple-element.8.member_ref, f32[8,128]{1,0:T(8,128)S(1)} %get-tuple-element.9.rewards_ref, s32[4,8]{1,0:T(4,128)S(1)} %pad_add_fusion.names_ref), custom_call_target="tpu_custom_call" | custom-call | tf_op jit(solution)/shard_map/finish/pallas_call | solution.py:302
  (12 shorter events, 0.1 us)
Async XLA Ops:
  1.4 0.9 %copy-start.2 = (bf16[8,2,3584]{2,1,0:T(2,128)(2,1)S(1)}, bf16[8,2,3584]{2,1,0:T(2,128)(2,1)}, u32[]{:S(2)}) copy-start(bf16[8,2,3584]{2,1,0:T(2,128)(2,1)} %hidden_ref.1) | copy-start | bytes 344068
  2.4 8.7 %collective-permute-start = (bf16[16,3712]{1,0:T(8,128)(2,1)S(1)}, bf16[16,3712]{1,0:T(8,128)(2,1)S(1)}, u32[]{:S(2)}, u32[]{:S(2)}) collective-permute-start(bf16[16,3712]{1,0:T(8,128)(2,1)S(1)} %prepare.1.own_ref.refs_0_), channel_id=1, source_target_pairs={{0,4},{1,5},{2,6},{3,7},{4,0},{5,1},{6,2},{7,3},{8,12},{9,13},{10,... | collective-permute-start | bytes 356360 | tf_op jit(solution)/shard_map/ppermute | solution.py:32
  5.5 5.6 %collective-permute-start.1 = (bf16[16,3712]{1,0:T(8,128)(2,1)S(1)}, bf16[16,3712]{1,0:T(8,128)(2,1)S(1)}, u32[]{:S(2)}, u32[]{:S(2)}) collective-permute-start(bf16[16,3712]{1,0:T(8,128)(2,1)S(1)} %prepare.1.own_ref.refs_0_), channel_id=1, source_target_pairs={{0,2},{1,17},{2,0},{3,19},{4,6},{5,21},{6,4},{7,23},{8,10},{9,25},... | collective-permute-start | bytes 356360 | tf_op jit(solution)/shard_map/ppermute | solution.py:32
  7.0 7.9 %collective-permute-start.4 = (bf16[16,3712]{1,0:T(8,128)(2,1)S(1)}, bf16[16,3712]{1,0:T(8,128)(2,1)S(1)}, u32[]{:S(2)}, u32[]{:S(2)}) collective-permute-start(bf16[16,3712]{1,0:T(8,128)(2,1)S(1)} %prepare.1.own_ref.refs_0_), channel_id=1, source_target_pairs={{0,8},{1,9},{2,10},{3,11},{4,12},{5,13},{6,14},{7,15},{8,0},{9,1},... | collective-permute-start | bytes 356360 | tf_op jit(solution)/shard_map/ppermute | solution.py:32
  9.6 6.8 %collective-permute-start.2 = (bf16[16,3712]{1,0:T(8,128)(2,1)S(1)}, bf16[16,3712]{1,0:T(8,128)(2,1)S(1)}, u32[]{:S(2)}, u32[]{:S(2)}) collective-permute-start(bf16[16,3712]{1,0:T(8,128)(2,1)S(1)} %prepare.1.own_ref.refs_0_), channel_id=1, source_target_pairs={{0,16},{1,3},{2,18},{3,1},{4,20},{5,7},{6,22},{7,5},{8,24},{9,11},... | collective-permute-start | bytes 356360 | tf_op jit(solution)/shard_map/ppermute | solution.py:32
  11.1 10.8 %collective-permute-start.3 = (bf16[32,3712]{1,0:T(8,128)(2,1)S(1)}, bf16[32,3712]{1,0:T(8,128)(2,1)S(1)}, u32[]{:S(2)}, u32[]{:S(2)}) collective-permute-start(bf16[32,3712]{1,0:T(8,128)(2,1)S(1)} %join.5), channel_id=1, source_target_pairs={{0,16},{1,3},{2,18},{3,1},{4,20},{5,7},{6,22},{7,5},{8,24},{9,11},... | collective-permute-start | bytes 712712 | tf_op jit(solution)/shard_map/ppermute | solution.py:32
  12.1 4.8 %collective-permute-start.5 = (bf16[16,3712]{1,0:T(8,128)(2,1)S(1)}, bf16[16,3712]{1,0:T(8,128)(2,1)S(1)}, u32[]{:S(2)}, u32[]{:S(2)}) collective-permute-start(bf16[16,3712]{1,0:T(8,128)(2,1)S(1)} %collective-permute-done.refs_1_.refs_0_), channel_id=1, source_target_pairs={{0,2},{1,17},{2,0},{3,19},{4,6},{5,21},{6,4},{7,23},{8,10},{9,25},... | collective-permute-start | bytes 356360 | tf_op jit(solution)/shard_map/ppermute | solution.py:32
  14.8 4.8 %collective-permute-start.9 = (bf16[16,3712]{1,0:T(8,128)(2,1)S(1)}, bf16[16,3712]{1,0:T(8,128)(2,1)S(1)}, u32[]{:S(2)}, u32[]{:S(2)}) collective-permute-start(bf16[16,3712]{1,0:T(8,128)(2,1)S(1)} %collective-permute-done.4.refs_0_), channel_id=1, source_target_pairs={{0,2},{1,17},{2,0},{3,19},{4,6},{5,21},{6,4},{7,23},{8,10},{9,25},... | collective-permute-start | bytes 356360 | tf_op jit(solution)/shard_map/ppermute | solution.py:32
  16.3 4.8 %collective-permute-start.10 = (bf16[16,3712]{1,0:T(8,128)(2,1)S(1)}, bf16[16,3712]{1,0:T(8,128)(2,1)S(1)}, u32[]{:S(2)}, u32[]{:S(2)}) collective-permute-start(bf16[16,3712]{1,0:T(8,128)(2,1)S(1)} %collective-permute-done.4.refs_0_), channel_id=1, source_target_pairs={{0,4},{1,5},{2,6},{3,7},{4,0},{5,1},{6,2},{7,3},{8,12},{9,13},{10,... | collective-permute-start | bytes 356360 | tf_op jit(solution)/shard_map/ppermute | solution.py:32
  16.4 16.9 %collective-permute-start.6 = (bf16[64,3712]{1,0:T(8,128)(2,1)S(1)}, bf16[64,3712]{1,0:T(8,128)(2,1)S(1)}, u32[]{:S(2)}, u32[]{:S(2)}) collective-permute-start(bf16[64,3712]{1,0:T(8,128)(2,1)S(1)} %join.4.refs_0_), channel_id=1, source_target_pairs={{0,1},{1,0},{2,3},{3,2},{4,5},{5,4},{6,7},{7,6},{8,9},{9,8},{10,11... | collective-permute-start | bytes 1425416 | tf_op jit(solution)/shard_map/ppermute | solution.py:32
  16.9 11.2 %collective-permute-start.8 = (bf16[32,3712]{1,0:T(8,128)(2,1)S(1)}, bf16[32,3712]{1,0:T(8,128)(2,1)S(1)}, u32[]{:S(2)}, u32[]{:S(2)}) collective-permute-start(bf16[32,3712]{1,0:T(8,128)(2,1)S(1)} %join.6.refs_2_), channel_id=1, source_target_pairs={{0,1},{1,0},{2,3},{3,2},{4,5},{5,4},{6,7},{7,6},{8,9},{9,8},{10,11... | collective-permute-start | bytes 712712 | tf_op jit(solution)/shard_map/ppermute | solution.py:32
  19.7 9.1 %collective-permute-start.11 = (bf16[32,3712]{1,0:T(8,128)(2,1)S(1)}, bf16[32,3712]{1,0:T(8,128)(2,1)S(1)}, u32[]{:S(2)}, u32[]{:S(2)}) collective-permute-start(bf16[32,3712]{1,0:T(8,128)(2,1)S(1)} %join.6.refs_2_), channel_id=1, source_target_pairs={{0,16},{1,3},{2,18},{3,1},{4,20},{5,7},{6,22},{7,5},{8,24},{9,11},... | collective-permute-start | bytes 712712 | tf_op jit(solution)/shard_map/ppermute | solution.py:32
  21.2 8.4 %collective-permute-start.15 = (bf16[32,3712]{1,0:T(8,128)(2,1)S(1)}, bf16[32,3712]{1,0:T(8,128)(2,1)S(1)}, u32[]{:S(2)}, u32[]{:S(2)}) collective-permute-start(bf16[32,3712]{1,0:T(8,128)(2,1)S(1)} %join.7.refs_0_), channel_id=1, source_target_pairs={{0,16},{1,3},{2,18},{3,1},{4,20},{5,7},{6,22},{7,5},{8,24},{9,11},... | collective-permute-start | bytes 712712 | tf_op jit(solution)/shard_map/ppermute | solution.py:32
  21.9 6.2 %collective-permute-start.14 = (bf16[16,3712]{1,0:T(8,128)(2,1)S(1)}, bf16[16,3712]{1,0:T(8,128)(2,1)}, u32[]{:S(2)}, u32[]{:S(2)}) collective-permute-start(bf16[16,3712]{1,0:T(8,128)(2,1)S(1)} %collective-permute-done.10.refs_1_), channel_id=1, source_target_pairs={{0,2},{1,17},{2,0},{3,19},{4,6},{5,21},{6,4},{7,23},{8,10},{9,25},... | collective-permute-start | bytes 356360 | tf_op jit(solution)/shard_map/ppermute | solution.py:32
  28.1 5.7 %collective-permute-start.7 = (bf16[32,3712]{1,0:T(8,128)(2,1)S(1)}, bf16[32,3712]{1,0:T(8,128)(2,1)S(1)}, u32[]{:S(2)}, u32[]{:S(2)}) collective-permute-start(bf16[32,3712]{1,0:T(8,128)(2,1)S(1)} %collective-permute-done.3.refs_1_), channel_id=1, source_target_pairs={{0,1},{1,0},{2,3},{3,2},{4,5},{5,4},{6,7},{7,6},{8,9},{9,8},{10,11... | collective-permute-start | bytes 712712 | tf_op jit(solution)/shard_map/ppermute | solution.py:32
  28.1 5.2 %collective-permute-start.16 = (bf16[16,3712]{1,0:T(8,128)(2,1)}, bf16[16,3712]{1,0:T(8,128)(2,1)}, u32[]{:S(2)}, u32[]{:S(2)}) collective-permute-start(bf16[16,3712]{1,0:T(8,128)(2,1)} %collective-permute-done.14.refs_3_), channel_id=1, source_target_pairs={{0,16},{1,3},{2,18},{3,1},{4,20},{5,7},{6,22},{7,5},{8,24},{9,11},... | collective-permute-start | bytes 356360 | tf_op jit(solution)/shard_map/ppermute | solution.py:32
  28.8 10.6 %collective-permute-start.12 = (bf16[32,3712]{1,0:T(8,128)(2,1)S(1)}, bf16[32,3712]{1,0:T(8,128)(2,1)S(1)}, u32[]{:S(2)}, u32[]{:S(2)}) collective-permute-start(bf16[32,3712]{1,0:T(8,128)(2,1)S(1)} %join.7.refs_0_), channel_id=1, source_target_pairs={{0,1},{1,0},{2,3},{3,2},{4,5},{5,4},{6,7},{7,6},{8,9},{9,8},{10,11... | collective-permute-start | bytes 712712 | tf_op jit(solution)/shard_map/ppermute | solution.py:32
  29.6 9.8 %collective-permute-start.13 = (bf16[32,3712]{1,0:T(8,128)(2,1)S(1)}, bf16[32,3712]{1,0:T(8,128)(2,1)S(1)}, u32[]{:S(2)}, u32[]{:S(2)}) collective-permute-start(bf16[32,3712]{1,0:T(8,128)(2,1)S(1)} %collective-permute-done.11.refs_1_), channel_id=1, source_target_pairs={{0,1},{1,0},{2,3},{3,2},{4,5},{5,4},{6,7},{7,6},{8,9},{9,8},{10,11... | collective-permute-start | bytes 712712 | tf_op jit(solution)/shard_map/ppermute | solution.py:32
  33.2 7.0 %collective-permute-start.18 = (bf16[32,3712]{1,0:T(8,128)(2,1)S(1)}, bf16[32,3712]{1,0:T(8,128)(2,1)S(1)}, u32[]{:S(2)}, u32[]{:S(2)}) collective-permute-start(bf16[32,3712]{1,0:T(8,128)(2,1)S(1)} %collective-permute-done.15.refs_4_), channel_id=1, source_target_pairs={{0,1},{1,0},{2,3},{3,2},{4,5},{5,4},{6,7},{7,6},{8,9},{9,8},{10,11... | collective-permute-start | bytes 712712 | tf_op jit(solution)/shard_map/ppermute | solution.py:32
  33.2 7.0 %collective-permute-start.17 = (bf16[16,3712]{1,0:T(8,128)(2,1)}, bf16[16,3712]{1,0:T(8,128)(2,1)}, u32[]{:S(2)}, u32[]{:S(2)}) collective-permute-start(bf16[16,3712]{1,0:T(8,128)(2,1)} %collective-permute-done.14.refs_3_), channel_id=1, source_target_pairs={{0,1},{1,0},{2,3},{3,2},{4,5},{5,4},{6,7},{7,6},{8,9},{9,8},{10,11... | collective-permute-start | bytes 356360 | tf_op jit(solution)/shard_map/ppermute | solution.py:32
  33.8 6.5 %collective-permute-start.19 = (bf16[16,3712]{1,0:T(8,128)(2,1)}, bf16[16,3712]{1,0:T(8,128)(2,1)}, u32[]{:S(2)}, u32[]{:S(2)}) collective-permute-start(bf16[16,3712]{1,0:T(8,128)(2,1)} %collective-permute-done.16.refs_5_), channel_id=1, source_target_pairs={{0,1},{1,0},{2,3},{3,2},{4,5},{5,4},{6,7},{7,6},{8,9},{9,8},{10,11... | collective-permute-start | bytes 356360 | tf_op jit(solution)/shard_map/ppermute | solution.py:32
  33.8 1.8 %copy-start = (bf16[3584,384]{1,0:T(8,128)(2,1)S(1)}, bf16[3584,384]{1,0:T(8,128)(2,1)}, u32[]{:S(2)}) copy-start(bf16[3584,384]{1,0:T(8,128)(2,1)} %head_ref.5) | copy-start | bytes 8257540
  35.6 0.7 %copy-start.3 = (bf16[3584]{0:T(1024)(128)(2,1)S(1)}, bf16[3584]{0:T(1024)(128)(2,1)}, u32[]{:S(2)}) copy-start(bf16[3584]{0:T(1024)(128)(2,1)} %param.8) | copy-start | bytes 21508
  36.3 1.8 %copy-start.1 = (bf16[3584,384]{1,0:T(8,128)(2,1)S(1)}, bf16[3584,384]{1,0:T(8,128)(2,1)}, u32[]{:S(2)}) copy-start(bf16[3584,384]{1,0:T(8,128)(2,1)} %head_ref.5) | copy-start | bytes 8257540
where the time goes:
time: 54.1 us; the launch traced here: 53.8 us
  starting transfers between devices  18 us (33%)
  waiting for transfers between devices  13.4 us (25%)
  blocking collectives  10.8 us (20%)
  Pallas kernels  5.25 us (10%)
  local copies, waits for them, and re-layouts  4.93 us (9%)
  between operations  0.73 us (1%)
  other arithmetic  0.72 us (1%)
    ppermute x20, starting transfers between devices, swap(): rows = lax.ppermute(piece.rows, AXES, pairs)  18 us
    ppermute x20, waiting for transfers between devices, swap(): rows = lax.ppermute(piece.rows, AXES, pairs)  13.4 us
    all_to_all x1, blocking collectives, body(): answer = lax.all_to_all(message, AXES, 0, 0, tiled=True)  10.8 us
    unnamed x8, local copies, waits for them, and re-layouts  4.93 us
    pallas_call x3, Pallas kernels, stats(): pl.pallas_call(functools.partial(stats_kernel, window=window, tokens=toke...  4.05 us
  transfers between devices with their start and end apart: 20, of which 7 were waited for; matrix products, arithmetic and copies ran while one was open for 0% of the time, Pallas kernels for 5%

commit v1 on v0

--- a/solution.py
+++ b/solution.py
@@ -82,12 +82,12 @@
     near_1 = swap(z1, one, devices)
     far_1 = swap(z2, one, devices)
     last_1 = swap(z3, one, devices)
-    second = join(z2, near_1)
-    second_2 = swap(second, two, devices)
-    third = join(far_1, z3)
+    far_3 = swap(z2, two, devices)
+    third = join(near_1, far_1, z3)
     third_2 = swap(third, two, devices)
     last_2 = swap(last_1, two, devices)
-    buckets = [[near, own_2, second], [third, second_2], [last_1, third_2, last_2]]
+    with_z2 = join(z2, far_3, third, last_1)
+    buckets = [[near, own_2], [with_z2], [third_2, last_2]]
     return [b + [swap(p, (1, 1), devices) for p in b] for b in buckets]
 
 

time: 54.1 us -> 62.3 us (1.15)
  waiting for transfers between devices: 13.4 us -> 21.3 us
  Pallas kernels: 5.25 us -> 8.59 us
  local copies, waits for them, and re-layouts: 4.93 us -> 1.8 us
  starting transfers between devices: 18 us -> 16.6 us
  blocking collectives: 10.8 us -> 12.1 us
    ppermute x20 -> x17, waiting for transfers between devices: 13.4 us -> 21.3 us  [swap(): rows = lax.ppermute(piece.rows, AXES, pairs)]
    unnamed x8 -> x10, local copies, waits for them, and re-layouts: 4.93 us -> 1.8 us
    pallas_call x3, Pallas kernels: 4.05 us -> 6.56 us  [stats(): pl.pallas_call(functools.partial(stats_kernel, window=window, tokens=toke...]
    ppermute x20 -> x17, starting transfers between devices: 18 us -> 16.6 us  [swap(): rows = lax.ppermute(piece.rows, AXES, pairs)]
    all_to_all x1, blocking collectives: 10.8 us -> 12.1 us  [body(): answer = lax.all_to_all(message, AXES, 0, 0, tiled=True)]
    pallas_call x4, Pallas kernels: 0.08 us -> 0.92 us  [join(): pl.pallas_call(join_kernel, out_shape=jax.ShapeDtypeStruct((count, width)...]
  transfers between devices with their start and end apart: 20 -> 17, of which waited for: 7 -> 10; matrix products, arithmetic and copies ran while one was open for 0% -> 0% of each run, Pallas kernels for 5% -> 9%
where the time goes in v1:
time: 62.3 us; the launch traced here: 62 us
  waiting for transfers between devices  21.3 us (34%)
  starting transfers between devices  16.6 us (27%)
  blocking collectives  12.1 us (19%)
  Pallas kernels  8.59 us (14%)
  local copies, waits for them, and re-layouts  1.8 us (3%)
  other arithmetic  0.87 us (1%)
  between operations  0.74 us (1%)
    ppermute x17, waiting for transfers between devices, swap(): rows = lax.ppermute(piece.rows, AXES, pairs)  21.3 us
    ppermute x17, starting transfers between devices, swap(): rows = lax.ppermute(piece.rows, AXES, pairs)  16.6 us
    all_to_all x1, blocking collectives, body(): answer = lax.all_to_all(message, AXES, 0, 0, tiled=True)  12.1 us
    pallas_call x3, Pallas kernels, stats(): pl.pallas_call(functools.partial(stats_kernel, window=window, tokens=toke...  6.56 us
    unnamed x10, local copies, waits for them, and re-layouts  1.8 us
  transfers between devices with their start and end apart: 17, of which 10 were waited for; matrix products, arithmetic and copies ran while one was open for 0% of the time, Pallas kernels for 9%

profile of v1, /device:TPU:0, one launch (start us, length us, event | category | flops | bytes accessed | tf_op | source)
XLA Modules:
  0.0 62.0 jit_solution(17260620873226871913)
XLA Ops:
  0.6 0.0 copy-start
  0.6 0.9 %pad_add_fusion.names_ref = s32[4,8]{1,0:T(4,128)S(1)} fusion(s32[1,8]{1,0:T(1,128)} %bitcast.15, s32[1,8]{1,0:T(1,128)} %bitcast.16, s32[2,8]{1,0:T(2,128)} %bitcast.14), kind=kLoop, calls=%fused_computation | loop fusion | flops 64 | bytes 256 | tf_op jit(solution)/shard_map/concatenate | solution.py:257
  1.5 0.9 %copy-done.3 = bf16[8,2,3584]{2,1,0:T(2,128)(2,1)S(1)} copy-done((bf16[8,2,3584]{2,1,0:T(2,128)(2,1)S(1)}, bf16[8,2,3584]{2,1,0:T(2,128)(2,1)}, u32[]{:S(2)}) %copy-start.3) | copy-done | bytes 114712
  2.4 0.1 prepare.1.own_ref.refs_0_
  2.5 0.0 copy-start.1
  2.5 4.1 %collective-permute-start.6 = (bf16[16,3712]{1,0:T(8,128)(2,1)S(1)}, bf16[16,3712]{1,0:T(8,128)(2,1)S(1)}, u32[]{:S(2)}, u32[]{:S(2)}) collective-permute-start(bf16[16,3712]{1,0:T(8,128)(2,1)S(1)} %prepare.1.own_ref.refs_0_), channel_id=1, source_target_pairs={{0,8},{1,9},{2,10},{3,11},{4,12},{5,13},{6,14},{7,15},{8,0},{9,1},... | collective-permute-start | bytes 356360 | tf_op jit(solution)/shard_map/ppermute | solution.py:32
  6.7 1.6 %collective-permute-start = (bf16[16,3712]{1,0:T(8,128)(2,1)S(1)}, bf16[16,3712]{1,0:T(8,128)(2,1)S(1)}, u32[]{:S(2)}, u32[]{:S(2)}) collective-permute-start(bf16[16,3712]{1,0:T(8,128)(2,1)S(1)} %prepare.1.own_ref.refs_0_), channel_id=1, source_target_pairs={{0,4},{1,5},{2,6},{3,7},{4,0},{5,1},{6,2},{7,3},{8,12},{9,13},{10,... | collective-permute-start | bytes 356360 | tf_op jit(solution)/shard_map/ppermute | solution.py:32
  8.2 4.3 %collective-permute-done.6.refs_0_ = bf16[16,3712]{1,0:T(8,128)(2,1)S(1)} collective-permute-done((bf16[16,3712]{1,0:T(8,128)(2,1)S(1)}, bf16[16,3712]{1,0:T(8,128)(2,1)S(1)}, u32[]{:S(2)}, u32[]{:S(2)}) %collective-permute-start.6) | collective-permute-done | bytes 118816 | tf_op jit(solution)/shard_map/ppermute | solution.py:32
  12.5 0.6 %collective-permute-start.10 = (bf16[16,3712]{1,0:T(8,128)(2,1)S(1)}, bf16[16,3712]{1,0:T(8,128)(2,1)S(1)}, u32[]{:S(2)}, u32[]{:S(2)}) collective-permute-start(bf16[16,3712]{1,0:T(8,128)(2,1)S(1)} %collective-permute-done.6.refs_0_), channel_id=1, source_target_pairs={{0,4},{1,5},{2,6},{3,7},{4,0},{5,1},{6,2},{7,3},{8,12},{9,13},{10,... | collective-permute-start | bytes 356360 | tf_op jit(solution)/shard_map/ppermute | solution.py:32
  13.2 0.0 collective-permute-done.refs_1_.refs_0_
  13.2 1.5 %collective-permute-start.8 = (bf16[16,3712]{1,0:T(8,128)(2,1)S(1)}, bf16[16,3712]{1,0:T(8,128)(2,1)S(1)}, u32[]{:S(2)}, u32[]{:S(2)}) collective-permute-start(bf16[16,3712]{1,0:T(8,128)(2,1)S(1)} %collective-permute-done.refs_1_.refs_0_), channel_id=1, source_target_pairs={{0,2},{1,17},{2,0},{3,19},{4,6},{5,21},{6,4},{7,23},{8,10},{9,25},... | collective-permute-start | bytes 356360 | tf_op jit(solution)/shard_map/ppermute | solution.py:32
  14.7 0.5 collective-permute-start.9
  15.2 1.5 %collective-permute-start.7 = (bf16[16,3712]{1,0:T(8,128)(2,1)S(1)}, bf16[16,3712]{1,0:T(8,128)(2,1)S(1)}, u32[]{:S(2)}, u32[]{:S(2)}) collective-permute-start(bf16[16,3712]{1,0:T(8,128)(2,1)S(1)} %collective-permute-done.6.refs_0_), channel_id=1, source_target_pairs={{0,16},{1,3},{2,18},{3,1},{4,20},{5,7},{6,22},{7,5},{8,24},{9,11},... | collective-permute-start | bytes 356360 | tf_op jit(solution)/shard_map/ppermute | solution.py:32
  16.7 0.7 %collective-permute-done.10.refs_2_ = bf16[16,3712]{1,0:T(8,128)(2,1)S(1)} collective-permute-done((bf16[16,3712]{1,0:T(8,128)(2,1)S(1)}, bf16[16,3712]{1,0:T(8,128)(2,1)S(1)}, u32[]{:S(2)}, u32[]{:S(2)}) %collective-permute-start.10) | collective-permute-done | bytes 118816 | tf_op jit(solution)/shard_map/ppermute | solution.py:32
  17.4 1.5 %collective-permute-start.11 = (bf16[16,3712]{1,0:T(8,128)(2,1)S(1)}, bf16[16,3712]{1,0:T(8,128)(2,1)S(1)}, u32[]{:S(2)}, u32[]{:S(2)}) collective-permute-start(bf16[16,3712]{1,0:T(8,128)(2,1)S(1)} %collective-permute-done.10.refs_2_), channel_id=1, source_target_pairs={{0,2},{1,17},{2,0},{3,19},{4,6},{5,21},{6,4},{7,23},{8,10},{9,25},... | collective-permute-start | bytes 356360 | tf_op jit(solution)/shard_map/ppermute | solution.py:32
  18.9 0.1 collective-permute-done.8.refs_0_
  19.0 1.5 %collective-permute-done.9.refs_1_ = bf16[16,3712]{1,0:T(8,128)(2,1)S(1)} collective-permute-done((bf16[16,3712]{1,0:T(8,128)(2,1)S(1)}, bf16[16,3712]{1,0:T(8,128)(2,1)S(1)}, u32[]{:S(2)}, u32[]{:S(2)}) %collective-permute-start.9) | collective-permute-done | bytes 118816 | tf_op jit(solution)/shard_map/ppermute | solution.py:32
  20.6 0.1 collective-permute-done.7.refs_1_
  20.7 1.5 %collective-permute-done.11.refs_3_ = bf16[16,3712]{1,0:T(8,128)(2,1)S(1)} collective-permute-done((bf16[16,3712]{1,0:T(8,128)(2,1)S(1)}, bf16[16,3712]{1,0:T(8,128)(2,1)S(1)}, u32[]{:S(2)}, u32[]{:S(2)}) %collective-permute-start.11) | collective-permute-done | bytes 118816 | tf_op jit(solution)/shard_map/ppermute | solution.py:32
  22.3 0.1 collective-permute-start.12
  22.3 1.6 %collective-permute-start.13 = (bf16[48,3712]{1,0:T(8,128)(2,1)S(1)}, bf16[48,3712]{1,0:T(8,128)(2,1)}, u32[]{:S(2)}, u32[]{:S(2)}) collective-permute-start(bf16[48,3712]{1,0:T(8,128)(2,1)S(1)} %join.6.refs_2_), channel_id=1, source_target_pairs={{0,16},{1,3},{2,18},{3,1},{4,20},{5,7},{6,22},{7,5},{8,24},{9,11},... | collective-permute-start | bytes 1069064 | tf_op jit(solution)/shard_map/ppermute | solution.py:32
  24.0 1.5 %collective-permute-start.1 = (bf16[16,3712]{1,0:T(8,128)(2,1)S(1)}, bf16[16,3712]{1,0:T(8,128)(2,1)S(1)}, u32[]{:S(2)}, u32[]{:S(2)}) collective-permute-start(bf16[16,3712]{1,0:T(8,128)(2,1)S(1)} %prepare.1.own_ref.refs_0_), channel_id=1, source_target_pairs={{0,2},{1,17},{2,0},{3,19},{4,6},{5,21},{6,4},{7,23},{8,10},{9,25},... | collective-permute-start | bytes 356360 | tf_op jit(solution)/shard_map/ppermute | solution.py:32
  25.5 0.5 collective-permute-start.2
  26.0 4.1 %collective-permute-done.1.refs_2_.refs_1_ = bf16[16,3712]{1,0:T(8,128)(2,1)S(1)} collective-permute-done((bf16[16,3712]{1,0:T(8,128)(2,1)S(1)}, bf16[16,3712]{1,0:T(8,128)(2,1)S(1)}, u32[]{:S(2)}, u32[]{:S(2)}) %collective-permute-start.1) | collective-permute-done | bytes 118816 | tf_op jit(solution)/shard_map/ppermute | solution.py:32
  30.1 0.5 collective-permute-start.3
  30.6 1.7 %collective-permute-done.2.refs_3_ = bf16[16,3712]{1,0:T(8,128)(2,1)S(1)} collective-permute-done((bf16[16,3712]{1,0:T(8,128)(2,1)S(1)}, bf16[16,3712]{1,0:T(8,128)(2,1)S(1)}, u32[]{:S(2)}, u32[]{:S(2)}) %collective-permute-start.2) | collective-permute-done | bytes 118816 | tf_op jit(solution)/shard_map/ppermute | solution.py:32
  32.3 0.8 %join.4.refs_0_ = bf16[64,3712]{1,0:T(8,128)(2,1)} custom-call(bf16[16,3712]{1,0:T(8,128)(2,1)S(1)} %prepare.1.own_ref.refs_0_, bf16[16,3712]{1,0:T(8,128)(2,1)S(1)} %collective-permute-done.refs_1_.refs_0_, bf16[16,3712]{1,0:T(8,128)(2,1)S(1)} %collective-permute-done.1.refs_2_.refs_1_, bf16[16,3712]{1,0:T(8,128)(2,1)S(1)} %collective-permute-done.2.refs_3_), custom_call_target="tpu_custom_call" | custom-call | flops 237568 | bytes 950272 | tf_op jit(solution)/shard_map/join/pallas_call | solution.py:52
  33.2 0.0 collective-permute-start.4
  33.2 0.0 collective-permute-done.13.refs_3_
  33.2 0.0 copy-done.1
  33.2 0.5 collective-permute-start.15
  33.7 2.7 %collective-permute-done.3.refs_1_ = bf16[32,3712]{1,0:T(8,128)(2,1)} collective-permute-done((bf16[32,3712]{1,0:T(8,128)(2,1)S(1)}, bf16[32,3712]{1,0:T(8,128)(2,1)}, u32[]{:S(2)}, u32[]{:S(2)}) %collective-permute-start.3) | collective-permute-done | bytes 237600 | tf_op jit(solution)/shard_map/ppermute | solution.py:32
  36.4 0.0 collective-permute-start.5
  36.4 0.5 collective-permute-start.14
  36.8 4.5 %collective-permute-done.14.refs_4_ = bf16[16,3712]{1,0:T(8,128)(2,1)} collective-permute-done((bf16[16,3712]{1,0:T(8,128)(2,1)S(1)}, bf16[16,3712]{1,0:T(8,128)(2,1)}, u32[]{:S(2)}, u32[]{:S(2)}) %collective-permute-start.14) | collective-permute-done | bytes 118816 | tf_op jit(solution)/shard_map/ppermute | solution.py:32
  41.3 0.0 collective-permute-start.16
  41.3 0.9 %copy-done.2 = bf16[16,3712]{1,0:T(8,128)(2,1)S(1)} copy-done((bf16[16,3712]{1,0:T(8,128)(2,1)S(1)}, bf16[16,3712]{1,0:T(8,128)(2,1)}, u32[]{:S(2)}) %copy-start.2) | copy-done | bytes 118808
  42.2 0.2 moments.1
  42.5 0.0 collective-permute-done.4.refs_2_
  42.5 0.0 collective-permute-done.5.refs_3_
  42.5 2.4 %stats.3.refs_1_ = f32[1,12,128]{2,1,0:T(8,128)S(1)} custom-call(s32[1]{0:T(128)} %bitcast.me_ref, bf16[3584,384]{1,0:T(8,128)(2,1)S(1)} %copy-done, bf16[64,3712]{1,0:T(8,128)(2,1)} %join.4.refs_0_, bf16[32,3712]{1,0:T(8,128)(2,1)} %collective-permute-done.3.refs_1_, bf16[64,3712]{1,0:T(8,128)(2,1)} %collective-permute-done.4.refs_2_, ...), custom_call_target="tpu_custom_call" | custom-call | flops 528482304 | bytes 2752512 | tf_op jit(solution)/shard_map/stats/pallas_call | solution.py:288
  44.9 0.0 collective-permute-done.12.refs_1_
  44.9 2.2 %stats.4.refs_2_ = f32[1,12,128]{2,1,0:T(8,128)S(1)} custom-call(s32[1]{0:T(128)} %bitcast.me_ref, bf16[3584,384]{1,0:T(8,128)(2,1)S(1)} %copy-done, bf16[96,3712]{1,0:T(8,128)(2,1)S(1)} %join.7.refs_0_, bf16[96,3712]{1,0:T(8,128)(2,1)} %collective-permute-done.12.refs_1_), custom_call_target="tpu_custom_call" | custom-call | flops 528482304 | bytes 2752512 | tf_op jit(solution)/shard_map/stats/pallas_call | solution.py:288
  47.0 0.0 collective-permute-done.16.refs_6_
  47.0 0.0 collective-permute-done.15.refs_5_
  47.1 2.0 %stats.5 = f32[32,128]{1,0:T(8,128)S(1)} custom-call(s32[1]{0:T(128)} %bitcast.me_ref, bf16[3584,384]{1,0:T(8,128)(2,1)S(1)} %copy-done, f32[1,128]{1,0:T(1,128)S(1)} %get-tuple-element.7.refs_0_, f32[1,12,128]{2,1,0:T(8,128)S(1)} %stats.3.refs_1_, f32[1,12,128]{2,1,0:T(8,128)S(1)} %stats.4.refs_2_, bf16[48,3712]{1,0:T(8,128)(2,1)} %collective-permute-done.13.refs_3_, ...), custom_call_target="tpu_custom_call" | custom-call | flops 352321536 | bytes 2752512 | tf_op jit(solution)/shard_map/stats/pallas_call | solution.py:288
  49.1 12.1 %all_to_all.11 = f32[32,1,128]{2,1,0:T(1,128)S(1)} all-to-all(f32[32,1,128]{2,1,0:T(1,128)S(1)} %bitcast.11), channel_id=1, replica_groups=mesh['rep'=2,'dp'=16] {'rep','dp'}, dimensions={0} | all-to-all | bytes 32768 | tf_op jit(solution)/shard_map/all_to_all | solution.py:301
  61.2 0.8 %finish.1 = (f32[2,8]{1,0:T(2,128)}, f32[1,8]{1,0:T(1,128)}) custom-call(f32[32,128]{1,0:T(8,128)S(1)} %bitcast.12, f32[8,128]{1,0:T(8,128)S(1)} %get-tuple-element.8.member_ref, f32[8,128]{1,0:T(8,128)S(1)} %get-tuple-element.9.rewards_ref, s32[4,8]{1,0:T(4,128)S(1)} %pad_add_fusion.names_ref), custom_call_target="tpu_custom_call" | custom-call | tf_op jit(solution)/shard_map/finish/pallas_call | solution.py:302
  (8 shorter events, 0.1 us)
Async XLA Ops:
  0.6 40.7 %copy-start = (bf16[3584,384]{1,0:T(8,128)(2,1)S(1)}, bf16[3584,384]{1,0:T(8,128)(2,1)}, u32[]{:S(2)}) copy-start(bf16[3584,384]{1,0:T(8,128)(2,1)} %head_ref.5) | copy-start | bytes 8257540
  1.5 0.9 %copy-start.3 = (bf16[8,2,3584]{2,1,0:T(2,128)(2,1)S(1)}, bf16[8,2,3584]{2,1,0:T(2,128)(2,1)}, u32[]{:S(2)}) copy-start(bf16[8,2,3584]{2,1,0:T(2,128)(2,1)} %hidden_ref.1) | copy-start | bytes 344068
  2.4 38.9 %copy-start.4 = (bf16[3584]{0:T(1024)(128)(2,1)S(1)}, bf16[3584]{0:T(1024)(128)(2,1)}, u32[]{:S(2)}) copy-start(bf16[3584]{0:T(1024)(128)(2,1)} %param.8) | copy-start | bytes 21508
  2.5 30.7 %copy-start.1 = (bf16[16,3712]{1,0:T(8,128)(2,1)}, bf16[16,3712]{1,0:T(8,128)(2,1)S(1)}, u32[]{:S(2)}) copy-start(bf16[16,3712]{1,0:T(8,128)(2,1)S(1)} %prepare.1.own_ref.refs_0_) | copy-start | bytes 356356
  2.5 10.0 %collective-permute-start.6 = (bf16[16,3712]{1,0:T(8,128)(2,1)S(1)}, bf16[16,3712]{1,0:T(8,128)(2,1)S(1)}, u32[]{:S(2)}, u32[]{:S(2)}) collective-permute-start(bf16[16,3712]{1,0:T(8,128)(2,1)S(1)} %prepare.1.own_ref.refs_0_), channel_id=1, source_target_pairs={{0,8},{1,9},{2,10},{3,11},{4,12},{5,13},{6,14},{7,15},{8,0},{9,1},... | collective-permute-start | bytes 356360 | tf_op jit(solution)/shard_map/ppermute | solution.py:32
  6.7 6.5 %collective-permute-start = (bf16[16,3712]{1,0:T(8,128)(2,1)S(1)}, bf16[16,3712]{1,0:T(8,128)(2,1)S(1)}, u32[]{:S(2)}, u32[]{:S(2)}) collective-permute-start(bf16[16,3712]{1,0:T(8,128)(2,1)S(1)} %prepare.1.own_ref.refs_0_), channel_id=1, source_target_pairs={{0,4},{1,5},{2,6},{3,7},{4,0},{5,1},{6,2},{7,3},{8,12},{9,13},{10,... | collective-permute-start | bytes 356360 | tf_op jit(solution)/shard_map/ppermute | solution.py:32
  12.5 4.8 %collective-permute-start.10 = (bf16[16,3712]{1,0:T(8,128)(2,1)S(1)}, bf16[16,3712]{1,0:T(8,128)(2,1)S(1)}, u32[]{:S(2)}, u32[]{:S(2)}) collective-permute-start(bf16[16,3712]{1,0:T(8,128)(2,1)S(1)} %collective-permute-done.6.refs_0_), channel_id=1, source_target_pairs={{0,4},{1,5},{2,6},{3,7},{4,0},{5,1},{6,2},{7,3},{8,12},{9,13},{10,... | collective-permute-start | bytes 356360 | tf_op jit(solution)/shard_map/ppermute | solution.py:32
  13.2 5.9 %collective-permute-start.8 = (bf16[16,3712]{1,0:T(8,128)(2,1)S(1)}, bf16[16,3712]{1,0:T(8,128)(2,1)S(1)}, u32[]{:S(2)}, u32[]{:S(2)}) collective-permute-start(bf16[16,3712]{1,0:T(8,128)(2,1)S(1)} %collective-permute-done.refs_1_.refs_0_), channel_id=1, source_target_pairs={{0,2},{1,17},{2,0},{3,19},{4,6},{5,21},{6,4},{7,23},{8,10},{9,25},... | collective-permute-start | bytes 356360 | tf_op jit(solution)/shard_map/ppermute | solution.py:32
  14.7 5.9 %collective-permute-start.9 = (bf16[16,3712]{1,0:T(8,128)(2,1)S(1)}, bf16[16,3712]{1,0:T(8,128)(2,1)S(1)}, u32[]{:S(2)}, u32[]{:S(2)}) collective-permute-start(bf16[16,3712]{1,0:T(8,128)(2,1)S(1)} %collective-permute-done.6.refs_0_), channel_id=1, source_target_pairs={{0,2},{1,17},{2,0},{3,19},{4,6},{5,21},{6,4},{7,23},{8,10},{9,25},... | collective-permute-start | bytes 356360 | tf_op jit(solution)/shard_map/ppermute | solution.py:32
  15.2 5.5 %collective-permute-start.7 = (bf16[16,3712]{1,0:T(8,128)(2,1)S(1)}, bf16[16,3712]{1,0:T(8,128)(2,1)S(1)}, u32[]{:S(2)}, u32[]{:S(2)}) collective-permute-start(bf16[16,3712]{1,0:T(8,128)(2,1)S(1)} %collective-permute-done.6.refs_0_), channel_id=1, source_target_pairs={{0,16},{1,3},{2,18},{3,1},{4,20},{5,7},{6,22},{7,5},{8,24},{9,11},... | collective-permute-start | bytes 356360 | tf_op jit(solution)/shard_map/ppermute | solution.py:32
  17.4 4.8 %collective-permute-start.11 = (bf16[16,3712]{1,0:T(8,128)(2,1)S(1)}, bf16[16,3712]{1,0:T(8,128)(2,1)S(1)}, u32[]{:S(2)}, u32[]{:S(2)}) collective-permute-start(bf16[16,3712]{1,0:T(8,128)(2,1)S(1)} %collective-permute-done.10.refs_2_), channel_id=1, source_target_pairs={{0,2},{1,17},{2,0},{3,19},{4,6},{5,21},{6,4},{7,23},{8,10},{9,25},... | collective-permute-start | bytes 356360 | tf_op jit(solution)/shard_map/ppermute | solution.py:32
  22.3 22.6 %collective-permute-start.12 = (bf16[96,3712]{1,0:T(8,128)(2,1)S(1)}, bf16[96,3712]{1,0:T(8,128)(2,1)}, u32[]{:S(2)}, u32[]{:S(2)}) collective-permute-start(bf16[96,3712]{1,0:T(8,128)(2,1)S(1)} %join.7.refs_0_), channel_id=1, source_target_pairs={{0,1},{1,0},{2,3},{3,2},{4,5},{5,4},{6,7},{7,6},{8,9},{9,8},{10,11... | collective-permute-start | bytes 2138120 | tf_op jit(solution)/shard_map/ppermute | solution.py:32
  22.3 10.8 %collective-permute-start.13 = (bf16[48,3712]{1,0:T(8,128)(2,1)S(1)}, bf16[48,3712]{1,0:T(8,128)(2,1)}, u32[]{:S(2)}, u32[]{:S(2)}) collective-permute-start(bf16[48,3712]{1,0:T(8,128)(2,1)S(1)} %join.6.refs_2_), channel_id=1, source_target_pairs={{0,16},{1,3},{2,18},{3,1},{4,20},{5,7},{6,22},{7,5},{8,24},{9,11},... | collective-permute-start | bytes 1069064 | tf_op jit(solution)/shard_map/ppermute | solution.py:32
  24.0 6.1 %collective-permute-start.1 = (bf16[16,3712]{1,0:T(8,128)(2,1)S(1)}, bf16[16,3712]{1,0:T(8,128)(2,1)S(1)}, u32[]{:S(2)}, u32[]{:S(2)}) collective-permute-start(bf16[16,3712]{1,0:T(8,128)(2,1)S(1)} %prepare.1.own_ref.refs_0_), channel_id=1, source_target_pairs={{0,2},{1,17},{2,0},{3,19},{4,6},{5,21},{6,4},{7,23},{8,10},{9,25},... | collective-permute-start | bytes 356360 | tf_op jit(solution)/shard_map/ppermute | solution.py:32
  25.5 6.9 %collective-permute-start.2 = (bf16[16,3712]{1,0:T(8,128)(2,1)S(1)}, bf16[16,3712]{1,0:T(8,128)(2,1)S(1)}, u32[]{:S(2)}, u32[]{:S(2)}) collective-permute-start(bf16[16,3712]{1,0:T(8,128)(2,1)S(1)} %prepare.1.own_ref.refs_0_), channel_id=1, source_target_pairs={{0,16},{1,3},{2,18},{3,1},{4,20},{5,7},{6,22},{7,5},{8,24},{9,11},... | collective-permute-start | bytes 356360 | tf_op jit(solution)/shard_map/ppermute | solution.py:32
  30.1 6.3 %collective-permute-start.3 = (bf16[32,3712]{1,0:T(8,128)(2,1)S(1)}, bf16[32,3712]{1,0:T(8,128)(2,1)}, u32[]{:S(2)}, u32[]{:S(2)}) collective-permute-start(bf16[32,3712]{1,0:T(8,128)(2,1)S(1)} %join.5), channel_id=1, source_target_pairs={{0,16},{1,3},{2,18},{3,1},{4,20},{5,7},{6,22},{7,5},{8,24},{9,11},... | collective-permute-start | bytes 712712 | tf_op jit(solution)/shard_map/ppermute | solution.py:32
  33.2 9.3 %collective-permute-start.4 = (bf16[64,3712]{1,0:T(8,128)(2,1)}, bf16[64,3712]{1,0:T(8,128)(2,1)}, u32[]{:S(2)}, u32[]{:S(2)}) collective-permute-start(bf16[64,3712]{1,0:T(8,128)(2,1)} %join.4.refs_0_), channel_id=1, source_target_pairs={{0,1},{1,0},{2,3},{3,2},{4,5},{5,4},{6,7},{7,6},{8,9},{9,8},{10,11... | collective-permute-start | bytes 1425416 | tf_op jit(solution)/shard_map/ppermute | solution.py:32
  33.2 13.9 %collective-permute-start.15 = (bf16[48,3712]{1,0:T(8,128)(2,1)}, bf16[48,3712]{1,0:T(8,128)(2,1)}, u32[]{:S(2)}, u32[]{:S(2)}) collective-permute-start(bf16[48,3712]{1,0:T(8,128)(2,1)} %collective-permute-done.13.refs_3_), channel_id=1, source_target_pairs={{0,1},{1,0},{2,3},{3,2},{4,5},{5,4},{6,7},{7,6},{8,9},{9,8},{10,11... | collective-permute-start | bytes 1069064 | tf_op jit(solution)/shard_map/ppermute | solution.py:32
  36.4 6.1 %collective-permute-start.5 = (bf16[32,3712]{1,0:T(8,128)(2,1)}, bf16[32,3712]{1,0:T(8,128)(2,1)}, u32[]{:S(2)}, u32[]{:S(2)}) collective-permute-start(bf16[32,3712]{1,0:T(8,128)(2,1)} %collective-permute-done.3.refs_1_), channel_id=1, source_target_pairs={{0,1},{1,0},{2,3},{3,2},{4,5},{5,4},{6,7},{7,6},{8,9},{9,8},{10,11... | collective-permute-start | bytes 712712 | tf_op jit(solution)/shard_map/ppermute | solution.py:32
  36.4 4.9 %collective-permute-start.14 = (bf16[16,3712]{1,0:T(8,128)(2,1)S(1)}, bf16[16,3712]{1,0:T(8,128)(2,1)}, u32[]{:S(2)}, u32[]{:S(2)}) collective-permute-start(bf16[16,3712]{1,0:T(8,128)(2,1)S(1)} %collective-permute-done.11.refs_3_), channel_id=1, source_target_pairs={{0,16},{1,3},{2,18},{3,1},{4,20},{5,7},{6,22},{7,5},{8,24},{9,11},... | collective-permute-start | bytes 356360 | tf_op jit(solution)/shard_map/ppermute | solution.py:32
  41.3 5.7 %collective-permute-start.16 = (bf16[16,3712]{1,0:T(8,128)(2,1)}, bf16[16,3712]{1,0:T(8,128)(2,1)}, u32[]{:S(2)}, u32[]{:S(2)}) collective-permute-start(bf16[16,3712]{1,0:T(8,128)(2,1)} %collective-permute-done.14.refs_4_), channel_id=1, source_target_pairs={{0,1},{1,0},{2,3},{3,2},{4,5},{5,4},{6,7},{7,6},{8,9},{9,8},{10,11... | collective-permute-start | bytes 356360 | tf_op jit(solution)/shard_map/ppermute | solution.py:32
  41.3 0.9 %copy-start.2 = (bf16[16,3712]{1,0:T(8,128)(2,1)S(1)}, bf16[16,3712]{1,0:T(8,128)(2,1)}, u32[]{:S(2)}) copy-start(bf16[16,3712]{1,0:T(8,128)(2,1)} %copy-done.1) | copy-start | bytes 356356

commit v2 on v1

--- a/solution.py
+++ b/solution.py
@@ -69,7 +69,7 @@
     stages = []
     for k in range(max(len(near), len(outer))):
         pair = near[k : k + 1] + outer[k : k + 1]
-        stages += [(pair[0], pair[-1]), (pair[-1], pair[0])][: len(pair)]
+        stages += [(pair[-1], pair[0]), (pair[0], pair[-1])][: len(pair)]
     *before, one, two = stages
     for masks in before:
         own = join(own, swap(own, masks, devices))
@@ -83,10 +83,11 @@
     far_1 = swap(z2, one, devices)
     last_1 = swap(z3, one, devices)
     far_3 = swap(z2, two, devices)
-    third = join(near_1, far_1, z3)
+    near_2 = swap(near_1, two, devices)
+    third = join(far_1, z3)
     third_2 = swap(third, two, devices)
     last_2 = swap(last_1, two, devices)
-    with_z2 = join(z2, far_3, third, last_1)
+    with_z2 = join(z2, far_3, near_1, near_2, third, last_1)
     buckets = [[near, own_2], [with_z2], [third_2, last_2]]
     return [b + [swap(p, (1, 1), devices) for p in b] for b in buckets]
 

time: 62.3 us -> 61.5 us (0.987)
  waiting for transfers between devices: 21.3 us -> 16.7 us
  starting transfers between devices: 16.6 us -> 20.7 us
  local copies, waits for them, and re-layouts: 1.8 us -> 0.91 us
    ppermute x17 -> x18, waiting for transfers between devices: 21.3 us -> 16.7 us  [swap(): rows = lax.ppermute(piece.rows, AXES, pairs)]
    ppermute x17 -> x18, starting transfers between devices: 16.6 us -> 20.7 us  [swap(): rows = lax.ppermute(piece.rows, AXES, pairs)]
    unnamed x10 -> x6, local copies, waits for them, and re-layouts: 1.8 us -> 0.91 us
  transfers between devices with their start and end apart: 17 -> 18, of which waited for: 10 -> 10; matrix products, arithmetic and copies ran while one was open for 0% -> 0% of each run, Pallas kernels for 9% -> 8%
where the time goes in v2:
time: 61.5 us; the launch traced here: 61.2 us
  starting transfers between devices  20.7 us (34%)
  waiting for transfers between devices  16.7 us (27%)
  blocking collectives  12.4 us (20%)
  Pallas kernels  8.88 us (14%)
  local copies, waits for them, and re-layouts  0.91 us (1%)
  other arithmetic  0.87 us (1%)
  between operations  0.73 us (1%)
    ppermute x18, starting transfers between devices, swap(): rows = lax.ppermute(piece.rows, AXES, pairs)  20.7 us
    ppermute x18, waiting for transfers between devices, swap(): rows = lax.ppermute(piece.rows, AXES, pairs)  16.7 us
    all_to_all x1, blocking collectives, body(): answer = lax.all_to_all(message, AXES, 0, 0, tiled=True)  12.4 us
    pallas_call x3, Pallas kernels, stats(): pl.pallas_call(functools.partial(stats_kernel, window=window, tokens=toke...  6.75 us
  transfers between devices with their start and end apart: 18, of which 10 were waited for; matrix products, arithmetic and copies ran while one was open for 0% of the time, Pallas kernels for 8%

profile of v2, /device:TPU:0, one launch (start us, length us, event | category | flops | bytes accessed | tf_op | source)
XLA Modules:
  0.0 61.2 jit_solution(3475653167596458056)
XLA Ops:
  0.6 0.0 copy-start
  0.6 0.9 %pad_add_fusion.names_ref = s32[4,8]{1,0:T(4,128)S(1)} fusion(s32[1,8]{1,0:T(1,128)} %bitcast.15, s32[1,8]{1,0:T(1,128)} %bitcast.16, s32[2,8]{1,0:T(2,128)} %bitcast.14), kind=kLoop, calls=%fused_computation | loop fusion | flops 64 | bytes 256 | tf_op jit(solution)/shard_map/concatenate | solution.py:258
  1.5 0.9 %copy-done.1 = bf16[8,2,3584]{2,1,0:T(2,128)(2,1)S(1)} copy-done((bf16[8,2,3584]{2,1,0:T(2,128)(2,1)S(1)}, bf16[8,2,3584]{2,1,0:T(2,128)(2,1)}, u32[]{:S(2)}) %copy-start.1) | copy-done | bytes 114712
  2.4 0.1 prepare.1.own_ref.refs_0_
  2.5 3.1 %collective-permute-start = (bf16[16,3712]{1,0:T(8,128)(2,1)S(1)}, bf16[16,3712]{1,0:T(8,128)(2,1)S(1)}, u32[]{:S(2)}, u32[]{:S(2)}) collective-permute-start(bf16[16,3712]{1,0:T(8,128)(2,1)S(1)} %prepare.1.own_ref.refs_0_), channel_id=1, source_target_pairs={{0,4},{1,5},{2,6},{3,7},{4,0},{5,1},{6,2},{7,3},{8,12},{9,13},{10,... | collective-permute-start | bytes 356360 | tf_op jit(solution)/shard_map/ppermute | solution.py:32
  5.6 2.6 %collective-permute-start.6 = (bf16[16,3712]{1,0:T(8,128)(2,1)S(1)}, bf16[16,3712]{1,0:T(8,128)(2,1)S(1)}, u32[]{:S(2)}, u32[]{:S(2)}) collective-permute-start(bf16[16,3712]{1,0:T(8,128)(2,1)S(1)} %prepare.1.own_ref.refs_0_), channel_id=1, source_target_pairs={{0,8},{1,9},{2,10},{3,11},{4,12},{5,13},{6,14},{7,15},{8,0},{9,1},... | collective-permute-start | bytes 356360 | tf_op jit(solution)/shard_map/ppermute | solution.py:32
  8.2 2.0 %collective-permute-done.refs_1_.refs_0_ = bf16[16,3712]{1,0:T(8,128)(2,1)S(1)} collective-permute-done((bf16[16,3712]{1,0:T(8,128)(2,1)S(1)}, bf16[16,3712]{1,0:T(8,128)(2,1)S(1)}, u32[]{:S(2)}, u32[]{:S(2)}) %collective-permute-start) | collective-permute-done | bytes 118816 | tf_op jit(solution)/shard_map/ppermute | solution.py:32
  10.2 1.8 %collective-permute-start.8 = (bf16[16,3712]{1,0:T(8,128)(2,1)S(1)}, bf16[16,3712]{1,0:T(8,128)(2,1)S(1)}, u32[]{:S(2)}, u32[]{:S(2)}) collective-permute-start(bf16[16,3712]{1,0:T(8,128)(2,1)S(1)} %collective-permute-done.refs_1_.refs_0_), channel_id=1, source_target_pairs={{0,16},{1,3},{2,18},{3,1},{4,20},{5,7},{6,22},{7,5},{8,24},{9,11},... | collective-permute-start | bytes 356360 | tf_op jit(solution)/shard_map/ppermute | solution.py:32
  12.0 1.8 %collective-permute-done.6.refs_0_ = bf16[16,3712]{1,0:T(8,128)(2,1)S(1)} collective-permute-done((bf16[16,3712]{1,0:T(8,128)(2,1)S(1)}, bf16[16,3712]{1,0:T(8,128)(2,1)S(1)}, u32[]{:S(2)}, u32[]{:S(2)}) %collective-permute-start.6) | collective-permute-done | bytes 118816 | tf_op jit(solution)/shard_map/ppermute | solution.py:32
  13.8 0.4 collective-permute-start.11
  14.3 1.5 %collective-permute-start.7 = (bf16[16,3712]{1,0:T(8,128)(2,1)S(1)}, bf16[16,3712]{1,0:T(8,128)(2,1)S(1)}, u32[]{:S(2)}, u32[]{:S(2)}) collective-permute-start(bf16[16,3712]{1,0:T(8,128)(2,1)S(1)} %collective-permute-done.6.refs_0_), channel_id=1, source_target_pairs={{0,2},{1,17},{2,0},{3,19},{4,6},{5,21},{6,4},{7,23},{8,10},{9,25},... | collective-permute-start | bytes 356360 | tf_op jit(solution)/shard_map/ppermute | solution.py:32
  15.8 1.5 %collective-permute-start.10 = (bf16[16,3712]{1,0:T(8,128)(2,1)S(1)}, bf16[16,3712]{1,0:T(8,128)(2,1)S(1)}, u32[]{:S(2)}, u32[]{:S(2)}) collective-permute-start(bf16[16,3712]{1,0:T(8,128)(2,1)S(1)} %collective-permute-done.6.refs_0_), channel_id=1, source_target_pairs={{0,16},{1,3},{2,18},{3,1},{4,20},{5,7},{6,22},{7,5},{8,24},{9,11},... | collective-permute-start | bytes 356360 | tf_op jit(solution)/shard_map/ppermute | solution.py:32
  17.3 0.0 collective-permute-done.8.refs_2_
  17.3 0.5 collective-permute-start.9
  17.8 0.8 %collective-permute-done.11.refs_1_ = bf16[16,3712]{1,0:T(8,128)(2,1)S(1)} collective-permute-done((bf16[16,3712]{1,0:T(8,128)(2,1)S(1)}, bf16[16,3712]{1,0:T(8,128)(2,1)S(1)}, u32[]{:S(2)}, u32[]{:S(2)}) %collective-permute-start.11) | collective-permute-done | bytes 118816 | tf_op jit(solution)/shard_map/ppermute | solution.py:32
  18.7 1.5 %collective-permute-start.12 = (bf16[16,3712]{1,0:T(8,128)(2,1)S(1)}, bf16[16,3712]{1,0:T(8,128)(2,1)S(1)}, u32[]{:S(2)}, u32[]{:S(2)}) collective-permute-start(bf16[16,3712]{1,0:T(8,128)(2,1)S(1)} %collective-permute-done.11.refs_1_), channel_id=1, source_target_pairs={{0,16},{1,3},{2,18},{3,1},{4,20},{5,7},{6,22},{7,5},{8,24},{9,11},... | collective-permute-start | bytes 356360 | tf_op jit(solution)/shard_map/ppermute | solution.py:32
  20.2 0.4 collective-permute-done.10.refs_0_
  20.6 0.0 collective-permute-done.7.refs_1_
  20.6 1.5 %collective-permute-done.9.refs_3_ = bf16[16,3712]{1,0:T(8,128)(2,1)S(1)} collective-permute-done((bf16[16,3712]{1,0:T(8,128)(2,1)S(1)}, bf16[16,3712]{1,0:T(8,128)(2,1)S(1)}, u32[]{:S(2)}, u32[]{:S(2)}) %collective-permute-start.9) | collective-permute-done | bytes 118816 | tf_op jit(solution)/shard_map/ppermute | solution.py:32
  22.1 1.4 %collective-permute-done.12.refs_5_ = bf16[16,3712]{1,0:T(8,128)(2,1)S(1)} collective-permute-done((bf16[16,3712]{1,0:T(8,128)(2,1)S(1)}, bf16[16,3712]{1,0:T(8,128)(2,1)S(1)}, u32[]{:S(2)}, u32[]{:S(2)}) %collective-permute-start.12) | collective-permute-done | bytes 118816 | tf_op jit(solution)/shard_map/ppermute | solution.py:32
  23.5 0.9 %join.7.refs_0_ = bf16[112,3712]{1,0:T(8,128)(2,1)} custom-call(bf16[16,3712]{1,0:T(8,128)(2,1)S(1)} %collective-permute-done.6.refs_0_, bf16[16,3712]{1,0:T(8,128)(2,1)S(1)} %collective-permute-done.7.refs_1_, bf16[16,3712]{1,0:T(8,128)(2,1)S(1)} %collective-permute-done.8.refs_2_, bf16[16,3712]{1,0:T(8,128)(2,1)S(1)} %collective-permute-done.9.refs_3_, ...), custom_call_target="tpu_custom_call" | custom-call | flops 415744 | bytes 1662976 | tf_op jit(solution)/shard_map/join/pallas_call | solution.py:52
  24.4 0.0 collective-permute-start.13
  24.4 1.5 %collective-permute-start.1 = (bf16[16,3712]{1,0:T(8,128)(2,1)S(1)}, bf16[16,3712]{1,0:T(8,128)(2,1)S(1)}, u32[]{:S(2)}, u32[]{:S(2)}) collective-permute-start(bf16[16,3712]{1,0:T(8,128)(2,1)S(1)} %prepare.1.own_ref.refs_0_), channel_id=1, source_target_pairs={{0,16},{1,3},{2,18},{3,1},{4,20},{5,7},{6,22},{7,5},{8,24},{9,11},... | collective-permute-start | bytes 356360 | tf_op jit(solution)/shard_map/ppermute | solution.py:32
  26.0 1.5 %collective-permute-start.2 = (bf16[16,3712]{1,0:T(8,128)(2,1)S(1)}, bf16[16,3712]{1,0:T(8,128)(2,1)S(1)}, u32[]{:S(2)}, u32[]{:S(2)}) collective-permute-start(bf16[16,3712]{1,0:T(8,128)(2,1)S(1)} %prepare.1.own_ref.refs_0_), channel_id=1, source_target_pairs={{0,2},{1,17},{2,0},{3,19},{4,6},{5,21},{6,4},{7,23},{8,10},{9,25},... | collective-permute-start | bytes 356360 | tf_op jit(solution)/shard_map/ppermute | solution.py:32
  27.5 2.3 %collective-permute-done.1.refs_2_.refs_1_ = bf16[16,3712]{1,0:T(8,128)(2,1)S(1)} collective-permute-done((bf16[16,3712]{1,0:T(8,128)(2,1)S(1)}, bf16[16,3712]{1,0:T(8,128)(2,1)S(1)}, u32[]{:S(2)}, u32[]{:S(2)}) %collective-permute-start.1) | collective-permute-done | bytes 118816 | tf_op jit(solution)/shard_map/ppermute | solution.py:32
  29.8 2.1 %collective-permute-start.3 = (bf16[32,3712]{1,0:T(8,128)(2,1)S(1)}, bf16[32,3712]{1,0:T(8,128)(2,1)}, u32[]{:S(2)}, u32[]{:S(2)}) collective-permute-start(bf16[32,3712]{1,0:T(8,128)(2,1)S(1)} %join.5), channel_id=1, source_target_pairs={{0,2},{1,17},{2,0},{3,19},{4,6},{5,21},{6,4},{7,23},{8,10},{9,25},... | collective-permute-start | bytes 712712 | tf_op jit(solution)/shard_map/ppermute | solution.py:32
  31.9 0.0 collective-permute-done.2.refs_3_
  32.0 0.1 collective-permute-start.4
  32.0 0.4 collective-permute-start.14
  32.5 3.6 %collective-permute-done.3.refs_1_ = bf16[32,3712]{1,0:T(8,128)(2,1)} collective-permute-done((bf16[32,3712]{1,0:T(8,128)(2,1)S(1)}, bf16[32,3712]{1,0:T(8,128)(2,1)}, u32[]{:S(2)}, u32[]{:S(2)}) %collective-permute-start.3) | collective-permute-done | bytes 237600 | tf_op jit(solution)/shard_map/ppermute | solution.py:32
  36.1 0.0 collective-permute-start.5
  36.1 2.0 %collective-permute-start.15 = (bf16[16,3712]{1,0:T(8,128)(2,1)S(1)}, bf16[16,3712]{1,0:T(8,128)(2,1)S(1)}, u32[]{:S(2)}, u32[]{:S(2)}) collective-permute-start(bf16[16,3712]{1,0:T(8,128)(2,1)S(1)} %collective-permute-done.12.refs_5_), channel_id=1, source_target_pairs={{0,2},{1,17},{2,0},{3,19},{4,6},{5,21},{6,4},{7,23},{8,10},{9,25},... | collective-permute-start | bytes 356360 | tf_op jit(solution)/shard_map/ppermute | solution.py:32
  38.1 0.5 collective-permute-done.14.refs_3_
  38.7 0.0 collective-permute-start.16
  38.7 2.3 %collective-permute-done.15.refs_4_ = bf16[16,3712]{1,0:T(8,128)(2,1)S(1)} collective-permute-done((bf16[16,3712]{1,0:T(8,128)(2,1)S(1)}, bf16[16,3712]{1,0:T(8,128)(2,1)S(1)}, u32[]{:S(2)}, u32[]{:S(2)}) %collective-permute-start.15) | collective-permute-done | bytes 118816 | tf_op jit(solution)/shard_map/ppermute | solution.py:32
  41.0 0.0 collective-permute-start.17
  41.0 0.0 copy-done
  41.0 0.2 moments.1
  41.2 0.0 collective-permute-done.4.refs_2_
  41.2 0.0 collective-permute-done.5.refs_3_
  41.2 2.2 %stats.3.refs_1_ = f32[1,12,128]{2,1,0:T(8,128)S(1)} custom-call(s32[1]{0:T(128)} %bitcast.me_ref, bf16[3584,384]{1,0:T(8,128)(2,1)S(1)} %copy-done, bf16[64,3712]{1,0:T(8,128)(2,1)S(1)} %join.4.refs_0_, bf16[32,3712]{1,0:T(8,128)(2,1)} %collective-permute-done.3.refs_1_, bf16[64,3712]{1,0:T(8,128)(2,1)} %collective-permute-done.4.refs_2_, ...), custom_call_target="tpu_custom_call" | custom-call | flops 528482304 | bytes 2752512 | tf_op jit(solution)/shard_map/stats/pallas_call | solution.py:289
  43.5 0.0 collective-permute-done.13.refs_1_
  43.5 2.6 %stats.4.refs_2_ = f32[1,14,128]{2,1,0:T(8,128)S(1)} custom-call(s32[1]{0:T(128)} %bitcast.me_ref, bf16[3584,384]{1,0:T(8,128)(2,1)S(1)} %copy-done, bf16[112,3712]{1,0:T(8,128)(2,1)} %join.7.refs_0_, bf16[112,3712]{1,0:T(8,128)(2,1)} %collective-permute-done.13.refs_1_), custom_call_target="tpu_custom_call" | custom-call | flops 616562688 | bytes 2752512 | tf_op jit(solution)/shard_map/stats/pallas_call | solution.py:289
  46.0 0.0 collective-permute-done.17.refs_6_
  46.0 0.0 collective-permute-done.16.refs_5_
  46.1 1.9 %stats.5 = f32[32,128]{1,0:T(8,128)S(1)} custom-call(s32[1]{0:T(128)} %bitcast.me_ref, bf16[3584,384]{1,0:T(8,128)(2,1)S(1)} %copy-done, f32[1,128]{1,0:T(1,128)S(1)} %get-tuple-element.7.refs_0_, f32[1,12,128]{2,1,0:T(8,128)S(1)} %stats.3.refs_1_, f32[1,14,128]{2,1,0:T(8,128)S(1)} %stats.4.refs_2_, bf16[32,3712]{1,0:T(8,128)(2,1)} %collective-permute-done.14.refs_3_, ...), custom_call_target="tpu_custom_call" | custom-call | flops 264241152 | bytes 2752512 | tf_op jit(solution)/shard_map/stats/pallas_call | solution.py:289
  48.0 12.4 %all_to_all.11 = f32[32,1,128]{2,1,0:T(1,128)S(1)} all-to-all(f32[32,1,128]{2,1,0:T(1,128)S(1)} %bitcast.11), channel_id=1, replica_groups=mesh['rep'=2,'dp'=16] {'rep','dp'}, dimensions={0} | all-to-all | bytes 32768 | tf_op jit(solution)/shard_map/all_to_all | solution.py:302
  60.4 0.8 %finish.1 = (f32[2,8]{1,0:T(2,128)}, f32[1,8]{1,0:T(1,128)}) custom-call(f32[32,128]{1,0:T(8,128)S(1)} %bitcast.12, f32[8,128]{1,0:T(8,128)S(1)} %get-tuple-element.8.member_ref, f32[8,128]{1,0:T(8,128)S(1)} %get-tuple-element.9.rewards_ref, s32[4,8]{1,0:T(4,128)S(1)} %pad_add_fusion.names_ref), custom_call_target="tpu_custom_call" | custom-call | tf_op jit(solution)/shard_map/finish/pallas_call | solution.py:303
  (6 shorter events, 0.1 us)
Async XLA Ops:
  0.6 40.3 %copy-start = (bf16[3584,384]{1,0:T(8,128)(2,1)S(1)}, bf16[3584,384]{1,0:T(8,128)(2,1)}, u32[]{:S(2)}) copy-start(bf16[3584,384]{1,0:T(8,128)(2,1)} %head_ref.5) | copy-start | bytes 8257540
  1.5 0.9 %copy-start.1 = (bf16[8,2,3584]{2,1,0:T(2,128)(2,1)S(1)}, bf16[8,2,3584]{2,1,0:T(2,128)(2,1)}, u32[]{:S(2)}) copy-start(bf16[8,2,3584]{2,1,0:T(2,128)(2,1)} %hidden_ref.1) | copy-start | bytes 344068
  2.4 38.6 %copy-start.2 = (bf16[3584]{0:T(1024)(128)(2,1)S(1)}, bf16[3584]{0:T(1024)(128)(2,1)}, u32[]{:S(2)}) copy-start(bf16[3584]{0:T(1024)(128)(2,1)} %param.8) | copy-start | bytes 21508
  2.5 7.7 %collective-permute-start = (bf16[16,3712]{1,0:T(8,128)(2,1)S(1)}, bf16[16,3712]{1,0:T(8,128)(2,1)S(1)}, u32[]{:S(2)}, u32[]{:S(2)}) collective-permute-start(bf16[16,3712]{1,0:T(8,128)(2,1)S(1)} %prepare.1.own_ref.refs_0_), channel_id=1, source_target_pairs={{0,4},{1,5},{2,6},{3,7},{4,0},{5,1},{6,2},{7,3},{8,12},{9,13},{10,... | collective-permute-start | bytes 356360 | tf_op jit(solution)/shard_map/ppermute | solution.py:32
  5.6 8.2 %collective-permute-start.6 = (bf16[16,3712]{1,0:T(8,128)(2,1)S(1)}, bf16[16,3712]{1,0:T(8,128)(2,1)S(1)}, u32[]{:S(2)}, u32[]{:S(2)}) collective-permute-start(bf16[16,3712]{1,0:T(8,128)(2,1)S(1)} %prepare.1.own_ref.refs_0_), channel_id=1, source_target_pairs={{0,8},{1,9},{2,10},{3,11},{4,12},{5,13},{6,14},{7,15},{8,0},{9,1},... | collective-permute-start | bytes 356360 | tf_op jit(solution)/shard_map/ppermute | solution.py:32
  10.2 7.1 %collective-permute-start.8 = (bf16[16,3712]{1,0:T(8,128)(2,1)S(1)}, bf16[16,3712]{1,0:T(8,128)(2,1)S(1)}, u32[]{:S(2)}, u32[]{:S(2)}) collective-permute-start(bf16[16,3712]{1,0:T(8,128)(2,1)S(1)} %collective-permute-done.refs_1_.refs_0_), channel_id=1, source_target_pairs={{0,16},{1,3},{2,18},{3,1},{4,20},{5,7},{6,22},{7,5},{8,24},{9,11},... | collective-permute-start | bytes 356360 | tf_op jit(solution)/shard_map/ppermute | solution.py:32
  13.8 4.8 %collective-permute-start.11 = (bf16[16,3712]{1,0:T(8,128)(2,1)S(1)}, bf16[16,3712]{1,0:T(8,128)(2,1)S(1)}, u32[]{:S(2)}, u32[]{:S(2)}) collective-permute-start(bf16[16,3712]{1,0:T(8,128)(2,1)S(1)} %collective-permute-done.6.refs_0_), channel_id=1, source_target_pairs={{0,4},{1,5},{2,6},{3,7},{4,0},{5,1},{6,2},{7,3},{8,12},{9,13},{10,... | collective-permute-start | bytes 356360 | tf_op jit(solution)/shard_map/ppermute | solution.py:32
  14.3 6.4 %collective-permute-start.7 = (bf16[16,3712]{1,0:T(8,128)(2,1)S(1)}, bf16[16,3712]{1,0:T(8,128)(2,1)S(1)}, u32[]{:S(2)}, u32[]{:S(2)}) collective-permute-start(bf16[16,3712]{1,0:T(8,128)(2,1)S(1)} %collective-permute-done.6.refs_0_), channel_id=1, source_target_pairs={{0,2},{1,17},{2,0},{3,19},{4,6},{5,21},{6,4},{7,23},{8,10},{9,25},... | collective-permute-start | bytes 356360 | tf_op jit(solution)/shard_map/ppermute | solution.py:32
  15.8 4.8 %collective-permute-start.10 = (bf16[16,3712]{1,0:T(8,128)(2,1)S(1)}, bf16[16,3712]{1,0:T(8,128)(2,1)S(1)}, u32[]{:S(2)}, u32[]{:S(2)}) collective-permute-start(bf16[16,3712]{1,0:T(8,128)(2,1)S(1)} %collective-permute-done.6.refs_0_), channel_id=1, source_target_pairs={{0,16},{1,3},{2,18},{3,1},{4,20},{5,7},{6,22},{7,5},{8,24},{9,11},... | collective-permute-start | bytes 356360 | tf_op jit(solution)/shard_map/ppermute | solution.py:32
  17.3 4.8 %collective-permute-start.9 = (bf16[16,3712]{1,0:T(8,128)(2,1)S(1)}, bf16[16,3712]{1,0:T(8,128)(2,1)S(1)}, u32[]{:S(2)}, u32[]{:S(2)}) collective-permute-start(bf16[16,3712]{1,0:T(8,128)(2,1)S(1)} %collective-permute-done.8.refs_2_), channel_id=1, source_target_pairs={{0,2},{1,17},{2,0},{3,19},{4,6},{5,21},{6,4},{7,23},{8,10},{9,25},... | collective-permute-start | bytes 356360 | tf_op jit(solution)/shard_map/ppermute | solution.py:32
  18.7 4.8 %collective-permute-start.12 = (bf16[16,3712]{1,0:T(8,128)(2,1)S(1)}, bf16[16,3712]{1,0:T(8,128)(2,1)S(1)}, u32[]{:S(2)}, u32[]{:S(2)}) collective-permute-start(bf16[16,3712]{1,0:T(8,128)(2,1)S(1)} %collective-permute-done.11.refs_1_), channel_id=1, source_target_pairs={{0,16},{1,3},{2,18},{3,1},{4,20},{5,7},{6,22},{7,5},{8,24},{9,11},... | collective-permute-start | bytes 356360 | tf_op jit(solution)/shard_map/ppermute | solution.py:32
  24.4 19.0 %collective-permute-start.13 = (bf16[112,3712]{1,0:T(8,128)(2,1)}, bf16[112,3712]{1,0:T(8,128)(2,1)}, u32[]{:S(2)}, u32[]{:S(2)}) collective-permute-start(bf16[112,3712]{1,0:T(8,128)(2,1)} %join.7.refs_0_), channel_id=1, source_target_pairs={{0,1},{1,0},{2,3},{3,2},{4,5},{5,4},{6,7},{7,6},{8,9},{9,8},{10,11... | collective-permute-start | bytes 2494472 | tf_op jit(solution)/shard_map/ppermute | solution.py:32
  24.4 5.4 %collective-permute-start.1 = (bf16[16,3712]{1,0:T(8,128)(2,1)S(1)}, bf16[16,3712]{1,0:T(8,128)(2,1)S(1)}, u32[]{:S(2)}, u32[]{:S(2)}) collective-permute-start(bf16[16,3712]{1,0:T(8,128)(2,1)S(1)} %prepare.1.own_ref.refs_0_), channel_id=1, source_target_pairs={{0,16},{1,3},{2,18},{3,1},{4,20},{5,7},{6,22},{7,5},{8,24},{9,11},... | collective-permute-start | bytes 356360 | tf_op jit(solution)/shard_map/ppermute | solution.py:32
  26.0 6.0 %collective-permute-start.2 = (bf16[16,3712]{1,0:T(8,128)(2,1)S(1)}, bf16[16,3712]{1,0:T(8,128)(2,1)S(1)}, u32[]{:S(2)}, u32[]{:S(2)}) collective-permute-start(bf16[16,3712]{1,0:T(8,128)(2,1)S(1)} %prepare.1.own_ref.refs_0_), channel_id=1, source_target_pairs={{0,2},{1,17},{2,0},{3,19},{4,6},{5,21},{6,4},{7,23},{8,10},{9,25},... | collective-permute-start | bytes 356360 | tf_op jit(solution)/shard_map/ppermute | solution.py:32
  29.8 6.3 %collective-permute-start.3 = (bf16[32,3712]{1,0:T(8,128)(2,1)S(1)}, bf16[32,3712]{1,0:T(8,128)(2,1)}, u32[]{:S(2)}, u32[]{:S(2)}) collective-permute-start(bf16[32,3712]{1,0:T(8,128)(2,1)S(1)} %join.5), channel_id=1, source_target_pairs={{0,2},{1,17},{2,0},{3,19},{4,6},{5,21},{6,4},{7,23},{8,10},{9,25},... | collective-permute-start | bytes 712712 | tf_op jit(solution)/shard_map/ppermute | solution.py:32
  32.0 9.2 %collective-permute-start.4 = (bf16[64,3712]{1,0:T(8,128)(2,1)S(1)}, bf16[64,3712]{1,0:T(8,128)(2,1)}, u32[]{:S(2)}, u32[]{:S(2)}) collective-permute-start(bf16[64,3712]{1,0:T(8,128)(2,1)S(1)} %join.4.refs_0_), channel_id=1, source_target_pairs={{0,1},{1,0},{2,3},{3,2},{4,5},{5,4},{6,7},{7,6},{8,9},{9,8},{10,11... | collective-permute-start | bytes 1425416 | tf_op jit(solution)/shard_map/ppermute | solution.py:32
  32.0 6.6 %collective-permute-start.14 = (bf16[32,3712]{1,0:T(8,128)(2,1)S(1)}, bf16[32,3712]{1,0:T(8,128)(2,1)}, u32[]{:S(2)}, u32[]{:S(2)}) collective-permute-start(bf16[32,3712]{1,0:T(8,128)(2,1)S(1)} %join.6.refs_4_), channel_id=1, source_target_pairs={{0,2},{1,17},{2,0},{3,19},{4,6},{5,21},{6,4},{7,23},{8,10},{9,25},... | collective-permute-start | bytes 712712 | tf_op jit(solution)/shard_map/ppermute | solution.py:32
  36.1 5.1 %collective-permute-start.5 = (bf16[32,3712]{1,0:T(8,128)(2,1)}, bf16[32,3712]{1,0:T(8,128)(2,1)}, u32[]{:S(2)}, u32[]{:S(2)}) collective-permute-start(bf16[32,3712]{1,0:T(8,128)(2,1)} %collective-permute-done.3.refs_1_), channel_id=1, source_target_pairs={{0,1},{1,0},{2,3},{3,2},{4,5},{5,4},{6,7},{7,6},{8,9},{9,8},{10,11... | collective-permute-start | bytes 712712 | tf_op jit(solution)/shard_map/ppermute | solution.py:32
  36.1 4.8 %collective-permute-start.15 = (bf16[16,3712]{1,0:T(8,128)(2,1)S(1)}, bf16[16,3712]{1,0:T(8,128)(2,1)S(1)}, u32[]{:S(2)}, u32[]{:S(2)}) collective-permute-start(bf16[16,3712]{1,0:T(8,128)(2,1)S(1)} %collective-permute-done.12.refs_5_), channel_id=1, source_target_pairs={{0,2},{1,17},{2,0},{3,19},{4,6},{5,21},{6,4},{7,23},{8,10},{9,25},... | collective-permute-start | bytes 356360 | tf_op jit(solution)/shard_map/ppermute | solution.py:32
  38.7 7.4 %collective-permute-start.16 = (bf16[32,3712]{1,0:T(8,128)(2,1)}, bf16[32,3712]{1,0:T(8,128)(2,1)}, u32[]{:S(2)}, u32[]{:S(2)}) collective-permute-start(bf16[32,3712]{1,0:T(8,128)(2,1)} %collective-permute-done.14.refs_3_), channel_id=1, source_target_pairs={{0,1},{1,0},{2,3},{3,2},{4,5},{5,4},{6,7},{7,6},{8,9},{9,8},{10,11... | collective-permute-start | bytes 712712 | tf_op jit(solution)/shard_map/ppermute | solution.py:32
  41.0 5.1 %collective-permute-start.17 = (bf16[16,3712]{1,0:T(8,128)(2,1)S(1)}, bf16[16,3712]{1,0:T(8,128)(2,1)}, u32[]{:S(2)}, u32[]{:S(2)}) collective-permute-start(bf16[16,3712]{1,0:T(8,128)(2,1)S(1)} %collective-permute-done.15.refs_4_), channel_id=1, source_target_pairs={{0,1},{1,0},{2,3},{3,2},{4,5},{5,4},{6,7},{7,6},{8,9},{9,8},{10,11... | collective-permute-start | bytes 356360 | tf_op jit(solution)/shard_map/ppermute | solution.py:32
